TPU v7x, 32 devices: a whole 2x2x4 slice. The times are simulated.
32 devices in a mesh: freq: 4 (over y, core), mesh: 8 (over z, x).
Axes of the slice: x: 2, y: 2, z: 4, core: 2. Of those that a mesh axis runs over, the one named last changes fastest.
Arguments:
- spectrum: float32 [2, 216, 32768], P(None, 'freq', 'mesh'), may hold values from -84 to 84
- time_weights: float32 [2, 432], P(None, 'freq'), may hold values from -0.625 to 0.625
- interp_weights: float32 [1024, 128, 128], P('mesh'), may hold values from -0.5 to 0.5
- group_block: int32 [1024], P('mesh'), may hold values from 0 to 255, as said below
- group_count: int32 [8], P('mesh'), may hold values from 64 to 128, as said below
- wave_state: float32 [4, 2, 524288], P('freq', None, 'mesh'), may hold values from -6 to 6
- neighbors: int32 [4, 4096], P(None, 'mesh'), may hold values from 0 to 575, as said below
- coupling: float32 [4, 524288], P(None, 'mesh'), may hold values from 0.02 to 0.2
Outputs:
- series: float32 [432, 32768], P('freq', 'mesh')
- new_state: float32 [4, 2, 524288], P('freq', None, 'mesh')
Inputs may be any that keep to these rules, and one draw needn't show every extreme that they name: `group_block`: partition o owns blocks o * 32 to o * 32 + 31. Of one partition's 128 groups at most 16 name blocks of one owner, and each partition has an owner named by exactly 16 of its live groups. The live groups of partition m are its first group_count[m]; some partition has exactly 128. `neighbors`: for the cell row with local row index u, a value e names local row e - 32 of the row's own partition when it lies in 32 .. (69632) // 128 - 1, else a row of the neighbouring partition below or above; never the row itself.
All inputs are finite; a program needn't handle non-finite values.
Results may differ from a plain program's by a relative error of at most 0.0001.
Values sent between devices are 32-bit elements; how exact they have to be, the bound alone decides.
A program may use at most 64 MiB of HBM per device.

v0:
```python
import functools
import math

import jax
import jax.numpy as jnp
import numpy as np
from jax import lax
from jax.experimental import pallas as pl
from jax.experimental.pallas import tpu as pltpu
from jax.sharding import PartitionSpec as P

LANE = 128
CORES = 2
HALO_CELLS = 4096
BLOCKS_PER_CHUNK = 4
EARLY = 2
HIGHEST = lax.Precision.HIGHEST
F32 = jnp.float32
BF16 = jnp.bfloat16


def pad8(n):
    return (n + 7) // 8 * 8


def split(x):
    high = x.astype(BF16)
    return high, (x - high.astype(F32)).astype(BF16)


def dot(a, b):
    return jnp.dot(a, b, preferred_element_type=F32)


def kernel(
    dims,
    count_smem,
    block_hbm,
    neigh_hbm,
    tw_hbm,
    basis_hbm,
    spec_hbm,
    weights_hbm,
    wave_hbm,
    coup_hbm,
    series_hbm,
    state_hbm,
    block_smem,
    neigh_smem,
    tw_own,
    basis_own,
    folded,
    own_spec,
    peer_spec,
    staged,
    lhs_high,
    lhs_low,
    cross_high,
    cross_low,
    raw,
    raw_peer,
    tw_all,
    own,
    outgoing,
    incoming,
    part,
    part_in,
    wall,
    picked,
    xt_high,
    xt_low,
    turned,
    weights,
    wave,
    coup,
    halo1,
    halo2,
    ext,
    gathered,
    state,
    spec_sem,
    swap_send,
    swap_recv,
    load_sem,
    tw_send,
    tw_recv,
    raw_send,
    raw_recv,
    pass_send,
    pass_recv,
    ser_send,
    ser_recv,
    part_send,
    part_recv,
    wall_send,
    wall_recv,
    halo_send,
    halo_recv,
    out_sem,
):
    ny, nm, coefs, rows, chunks = dims
    groups = weights.shape[0]
    kp, rp = pad8(coefs), pad8(rows)
    m1 = ny * rp
    per = part.shape[1] // 2
    cell_rows = ext.shape[0] - 2 * halo1.shape[1] // 2
    halo = halo1.shape[1] // 2
    width = BLOCKS_PER_CHUNK * LANE
    seg = 2 * BLOCKS_PER_CHUNK

    freq = lax.axis_index("freq")
    me = lax.axis_index("mesh")
    chip, core = freq // CORES, freq % CORES
    partner = chip * CORES + (1 - core)

    def at_chip(d):
        return ((chip + d + ny) % ny) * CORES + core

    def peer(d):
        return (me + d + nm) % nm

    def remote(src, dst, send, recv, axis, target):
        return pltpu.make_async_remote_copy(
            src_ref=src,
            dst_ref=dst,
            send_sem=send,
            recv_sem=recv,
            device_id={axis: target},
            device_id_type=pl.DeviceIdType.MESH,
        )

    def load_spec(c):
        return pltpu.make_async_copy(
            spec_hbm.at[:, pl.ds(c * seg, seg), :], own_spec.at[c], spec_sem.at[c]
        )

    def swap(c):
        return remote(
            spec_hbm.at[:, pl.ds(c * seg, seg), :],
            peer_spec.at[c],
            swap_send.at[c],
            swap_recv.at[c],
            "freq",
            partner,
        )

    def send_tw(d):
        return remote(
            tw_own, tw_all.at[d - 1], tw_send.at[d - 1], tw_recv.at[d - 1], "freq", at_chip(-d)
        )

    def send_raw(d):
        return remote(
            spec_hbm.at[:, pl.ds((chunks - 1) * seg, seg), :],
            raw.at[d - 1],
            raw_send.at[d - 1],
            raw_recv.at[d - 1],
            "freq",
            at_chip(d),
        )

    def pass_raw(d):
        return remote(
            raw.at[d - 1],
            raw_peer.at[d - 1],
            pass_send.at[d - 1],
            pass_recv.at[d - 1],
            "freq",
            partner,
        )

    def send_series(d, c):
        return remote(
            outgoing.at[d - 1, c],
            incoming.at[d - 1, c],
            ser_send.at[d - 1, c],
            ser_recv.at[d - 1, c],
            "freq",
            at_chip(d),
        )

    def send_part(d):
        return remote(
            part.at[d],
            part_in.at[d - 1],
            part_send.at[d - 1],
            part_recv.at[d - 1],
            "freq",
            at_chip(d),
        )

    def send_wall(o):
        mine = pl.ds(pl.multiple_of(me * 2 * per, 8), 2 * per)
        return remote(
            wall.at[mine], wall.at[mine], wall_send.at[o - 1], wall_recv.at[o - 1], "mesh", peer(o)
        )

    def send_halo1(side):
        first = 0 if side else 2 * (cell_rows - halo)
        return remote(
            wave.at[pl.ds(first, 2 * halo)],
            halo1.at[side],
            halo_send.at[side],
            halo_recv.at[side],
            "mesh",
            peer(-1 if side else 1),
        )

    def send_halo2(side):
        first = halo if side else cell_rows
        return remote(
            ext.at[pl.ds(first, halo)],
            halo2.at[side],
            halo_send.at[2 + side],
            halo_recv.at[2 + side],
            "mesh",
            peer(-1 if side else 1),
        )

    def store_series(c):
        return pltpu.make_async_copy(
            own.at[c], series_hbm.at[:, pl.ds(pl.multiple_of(c * width, width), width)], out_sem.at[c]
        )

    load_wave = pltpu.make_async_copy(wave_hbm, wave, load_sem.at[0])
    load_coup = pltpu.make_async_copy(coup_hbm, coup, load_sem.at[1])
    load_weights = pltpu.make_async_copy(weights_hbm, weights, load_sem.at[2])

    load_tw = pltpu.make_async_copy(tw_hbm, tw_own, load_sem.at[4])
    load_basis = pltpu.make_async_copy(basis_hbm.at[freq], basis_own, load_sem.at[5])
    load_neigh = pltpu.make_async_copy(neigh_hbm, neigh_smem, load_sem.at[6])
    load_block = pltpu.make_async_copy(block_hbm, block_smem, load_sem.at[7])

    load_tw.start()
    load_basis.start()
    for c in range(chunks):
        load_spec(c).start()
    load_wave.start()
    load_neigh.start()
    load_block.start()

    barrier = pltpu.get_barrier_semaphore()
    pl.semaphore_signal(
        barrier, inc=1, device_id={"freq": partner}, device_id_type=pl.DeviceIdType.MESH
    )
    for d in range(1, ny):
        pl.semaphore_signal(
            barrier, inc=1, device_id={"freq": at_chip(d)}, device_id_type=pl.DeviceIdType.MESH
        )
    for o in range(1, nm):
        pl.semaphore_signal(
            barrier, inc=1, device_id={"mesh": peer(o)}, device_id_type=pl.DeviceIdType.MESH
        )
    pl.semaphore_wait(barrier, 1 + (ny - 1) + (nm - 1))

    swap(0).start()
    load_tw.wait()
    for d in range(1, ny):
        send_tw(d).start()
    for d in range(1, ny):
        send_raw(d).start()
    for c in range(1, chunks):
        swap(c).start()
    load_coup.start()
    load_weights.start()

    staged[...] = jnp.zeros_like(staged)
    folded[...] = jnp.zeros_like(folded)
    load_basis.wait()
    high, low = split(basis_own[0:m1, :])
    lhs_high[0:m1, :] = high
    lhs_low[0:m1, :] = low
    load_wave.wait()
    for side in range(2):
        send_halo1(side).start()

    own_rows = own_spec.reshape(chunks * coefs * seg, LANE)
    peer_rows = peer_spec.reshape(chunks * coefs * seg, LANE)

    raw_rows = raw.reshape(max(ny - 1, 1) * coefs * seg, LANE)
    raw_peer_rows = raw_peer.reshape(max(ny - 1, 1) * coefs * seg, LANE)

    def stage(sources, c):
        for p, source in enumerate(sources):
            for s in range(2):
                for j in range(BLOCKS_PER_CHUNK):
                    piece = source[pl.ds(c * (coefs * seg) + 2 * j + s, coefs, stride=seg), :]
                    base = (p * 2 + s) * kp
                    staged[base : base + coefs, j * LANE : (j + 1) * LANE] = piece
        return split(staged[...])

    def stage_chunk(c):
        load_spec(c).wait()
        swap(c).wait_recv()
        return stage((own_rows, peer_rows), c)

    def product(first, last, s_high, s_low):
        high = lhs_high[first:last, :]
        return dot(high, s_high) + dot(lhs_low[first:last, :], s_high) + dot(high, s_low)

    def keep_series(c, total):
        own[c] = total[0:rows]
        for d in range(1, ny):
            outgoing[d - 1, c] = total[d * rp : d * rp + rows]

    def keep_part(c, total):
        for d in range(ny):
            for s in range(2):
                row = 8 * d + s
                for j in range(BLOCKS_PER_CHUNK):
                    part[d, pl.ds(s * per + c * BLOCKS_PER_CHUNK + j, 1), :] = total[
                        row : row + 1, j * LANE : (j + 1) * LANE
                    ]

    m_all = m1 + 8 * ny
    s_high, s_low = stage_chunk(0)
    keep_series(0, product(0, m1, s_high, s_low))
    for d in range(1, ny):
        send_series(d, 0).start()
    for d in range(ny):
        if d:
            send_tw(d).wait_recv()
        tw = tw_all[d - 1] if d else tw_own[...]
        folded[8 * d : 8 * d + 2, :] = jnp.dot(
            tw,
            basis_own[d * rp : d * rp + rows, :],
            precision=HIGHEST,
            preferred_element_type=F32,
        )
    high, low = split(folded[...])
    lhs_high[m1:, :] = high
    lhs_low[m1:, :] = low
    keep_part(0, product(m1, m_all, s_high, s_low))

    def partial_chunk(c, carry):
        s_high, s_low = stage_chunk(c)
        total = product(0, m_all, s_high, s_low)
        keep_series(c, total)
        keep_part(c, total[m1:])

        @pl.when(c < EARLY)
        def _():
            for d in range(1, ny):
                send_series(d, c).start()

        return carry

    lax.fori_loop(1, chunks, partial_chunk, 0)
    for d in range(1, ny):
        send_part(d).start()

    def later(c, carry):
        for d in range(1, ny):
            send_series(d, c).start()
        return carry

    lax.fori_loop(EARLY, chunks - 1, later, 0)
    for d in range(1, ny):
        send_raw(d).wait_recv()
        pass_raw(d).start()

    wave_rows = 64

    def stage_current(b, carry):
        at = b * wave_rows
        ext[pl.ds(halo + at, wave_rows), :] = wave[pl.ds(2 * at + 1, wave_rows, stride=2), :]
        return carry

    lax.fori_loop(0, cell_rows // wave_rows, stage_current, 0)

    load_neigh.wait()
    load_block.wait()

    def gather():
        def tile(t, carry):
            for n in range(4):
                for i in range(8):
                    u = t * 8 + i
                    gathered[n, pl.ds(u, 1), :] = ext[pl.ds(neigh_smem[n, u], 1), :]
            return carry

        lax.fori_loop(0, cell_rows // 8, tile, 0)

    def spread_of(at, center):
        total = jnp.zeros((wave_rows, LANE), F32)
        for n in range(4):
            factor = coup[pl.ds(4 * at + n, wave_rows, stride=4), :]
            total += factor * (gathered[n, pl.ds(at, wave_rows), :] - center)
        return total

    inside_low = (jnp.zeros((halo, LANE), jnp.int32) + me) > 0
    inside_high = (jnp.zeros((halo, LANE), jnp.int32) + me) < nm - 1

    for side in range(2):
        send_halo1(side).wait_recv()
    ext[0:halo, :] = jnp.where(inside_low, halo1[0, pl.ds(1, halo, stride=2), :], 0.0)
    ext[halo + cell_rows :, :] = jnp.where(
        inside_high, halo1[1, pl.ds(1, halo, stride=2), :], 0.0
    )
    load_coup.wait()

    for d in range(1, ny):
        send_part(d).wait_recv()
    weighted = part[0]
    for d in range(1, ny):
        weighted += part_in[d - 1]
    wall[pl.ds(pl.multiple_of(me * 2 * per, 8), 2 * per), :] = weighted
    for o in range(1, nm):
        send_wall(o).start()

    gather()

    def first_step(b, carry):
        at = b * wave_rows
        center = ext[pl.ds(halo + at, wave_rows), :]
        previous = wave[pl.ds(2 * at, wave_rows, stride=2), :]
        state[pl.ds(2 * at, wave_rows, stride=2), :] = (
            2.0 * center - previous + spread_of(at, center)
        )
        return carry

    lax.fori_loop(0, cell_rows // wave_rows, first_step, 0)

    total = own[chunks - 1]
    for d in range(1, ny):
        high, low = split(basis_own[m1 + (d - 1) * rp : m1 + d * rp, :])
        cross_high[d - 1] = high
        cross_low[d - 1] = low
        pass_raw(d).wait_recv()
        s_high, s_low = stage((raw_rows, raw_peer_rows), d - 1)
        high = cross_high[d - 1]
        product_d = dot(high, s_high) + dot(cross_low[d - 1], s_high) + dot(high, s_low)
        total += product_d[0:rows]
    own[chunks - 1] = total
    store_series(chunks - 1).start()

    for o in range(1, nm):
        send_wall(o).wait_recv()

    def pick(t, carry):
        for i in range(8):
            g = t * 8 + i
            block = block_smem[g]
            row = (block // per) * (2 * per) + block % per
            picked[pl.ds(g, 1), :] = wall[pl.ds(row, 1), :]
            picked[pl.ds(groups + g, 1), :] = wall[pl.ds(row + per, 1), :]
        return carry

    lax.fori_loop(0, groups // 8, pick, 0)
    high, low = split(picked[...].T)
    xt_high[0:LANE, :] = high
    xt_high[LANE:, :] = high
    xt_low[...] = low
    load_weights.wait()
    batch = 8
    lane = lax.broadcasted_iota(jnp.int32, (LANE, groups), 1)

    def interpolate(t, carry):
        block = weights[pl.ds(t * batch, batch)].reshape(batch * LANE, LANE)
        w_high, w_low = split(block)
        both = jnp.concatenate([w_high, w_low], axis=1)
        result = dot(both, xt_high[...]) + dot(w_high, xt_low[...])
        for s in range(2):
            column = turned[s]
            for i in range(batch):
                column = jnp.where(
                    lane == t * batch + i,
                    result[i * LANE : (i + 1) * LANE, s * groups : (s + 1) * groups],
                    column,
                )
            turned[s] = column
        return carry

    turned[...] = jnp.zeros_like(turned)
    lax.fori_loop(0, groups // batch, interpolate, 0)
    alive = lax.broadcasted_iota(jnp.int32, (groups, LANE), 0) < count_smem[0]
    push = [jnp.where(alive, turned[s].T, 0.0) for s in range(2)]

    top = pl.ds(0, groups, stride=2)
    state[top, :] = state[top, :] + push[0]

    def stage_stepped(b, carry):
        at = b * wave_rows
        ext[pl.ds(halo + at, wave_rows), :] = state[pl.ds(2 * at, wave_rows, stride=2), :]
        return carry

    lax.fori_loop(0, cell_rows // wave_rows, stage_stepped, 0)
    for side in range(2):
        send_halo2(side).start()
    for side in range(2):
        send_halo2(side).wait_recv()
    ext[0:halo, :] = jnp.where(inside_low, halo2[0], 0.0)
    ext[halo + cell_rows :, :] = jnp.where(inside_high, halo2[1], 0.0)
    gather()

    def second_step(b, carry):
        at = b * wave_rows
        center = ext[pl.ds(halo + at, wave_rows), :]
        previous = wave[pl.ds(2 * at + 1, wave_rows, stride=2), :]
        state[pl.ds(2 * at + 1, wave_rows, stride=2), :] = (
            2.0 * center - previous + spread_of(at, center)
        )
        return carry

    lax.fori_loop(0, cell_rows // wave_rows, second_step, 0)
    bottom = pl.ds(1, groups, stride=2)
    state[bottom, :] = state[bottom, :] + push[1]
    store_state = pltpu.make_async_copy(state, state_hbm, load_sem.at[3])
    store_state.start()

    def finish(c, carry):
        total = own[c]
        for d in range(1, ny):
            send_series(d, c).wait_recv()
            total += incoming[d - 1, c]
        own[c] = total
        store_series(c).start()
        return carry

    lax.fori_loop(0, chunks - 1, finish, 0)

    def drain(c, carry):
        swap(c).wait_send()
        for d in range(1, ny):
            send_series(d, c).wait_send()
        store_series(c).wait()
        return carry

    lax.fori_loop(0, chunks - 1, drain, 0)
    swap(chunks - 1).wait_send()
    store_series(chunks - 1).wait()
    for d in range(1, ny):
        send_raw(d).wait_send()
        pass_raw(d).wait_send()
        send_tw(d).wait_send()
        send_part(d).wait_send()
    for o in range(1, nm):
        send_wall(o).wait_send()
    for side in range(2):
        send_halo1(side).wait_send()
        send_halo2(side).wait_send()
    store_state.wait()


def chip_basis(ny, coefs, rows, horizon):
    kp, rp = pad8(coefs), pad8(rows)
    freq = np.arange(ny * CORES).reshape(-1, 1, 1, 1, 1, 1)
    d, r, p, s, k = np.indices((2 * ny - 1, rp, CORES, 2, kp), sparse=True)
    chip, core = freq // CORES, freq % CORES
    source = chip - np.where(d < ny, 0, d - ny + 1)
    window = ((chip + np.where(d < ny, d, 0)) % ny) * CORES + core
    wave_number = (source % ny * CORES + (core + p) % CORES) * coefs + k
    angle = ((window * rows + r) * wave_number) % horizon * (2.0 * math.pi / horizon)
    scale = np.where(wave_number == 0, 1.0, 2.0) / horizon
    value = np.where(s == 0, np.cos(angle), -np.sin(angle)) * scale
    value = np.where((r < rows) & (k < coefs), value, 0.0)
    return value.reshape(ny * CORES, (2 * ny - 1) * rp, CORES * 2 * kp).astype(np.float32)


def local(
    ny,
    nm,
    spectrum,
    time_weights,
    interp_weights,
    group_block,
    group_count,
    wave_state,
    neighbors,
    coupling,
):
    coefs, points = spectrum.shape[1:]
    rows = time_weights.shape[1]
    horizon = rows * ny * CORES
    groups = interp_weights.shape[0]
    cell_rows = neighbors.shape[1]
    halo = HALO_CELLS // LANE
    blocks = points // LANE
    chunks = blocks // BLOCKS_PER_CHUNK
    kp, rp = pad8(coefs), pad8(rows)
    k_all, m_all = CORES * 2 * kp, ny * (rp + 8)
    seg = 2 * BLOCKS_PER_CHUNK
    width = BLOCKS_PER_CHUNK * LANE

    spec = spectrum.reshape(2, coefs, blocks, LANE).transpose(1, 2, 0, 3)
    spec = spec.reshape(coefs, 2 * blocks, LANE)
    wave = wave_state.reshape(2, cell_rows, LANE).transpose(1, 0, 2).reshape(2 * cell_rows, LANE)
    coup = coupling.reshape(4, cell_rows, LANE).transpose(1, 0, 2).reshape(4 * cell_rows, LANE)
    basis = jnp.asarray(chip_basis(ny, coefs, rows, horizon))

    vmem = lambda *shape: pltpu.VMEM(shape, F32)
    dma = lambda *shape: pltpu.SemaphoreType.DMA(shape)
    smem = pl.BlockSpec(memory_space=pltpu.SMEM)
    hbm = pl.BlockSpec(memory_space=pltpu.HBM)
    any_space = pl.BlockSpec(memory_space=pl.ANY)
    far = max(ny - 1, 1)
    pinned = [
        pltpu.with_memory_space_constraint(x, pltpu.HBM)
        for x in (
            group_block,
            neighbors,
            time_weights,
            basis,
            spec,
            interp_weights,
            wave,
            coup,
        )
    ]
    series, state = pl.pallas_call(
        functools.partial(kernel, (ny, nm, coefs, rows, chunks)),
        out_shape=(
            jax.ShapeDtypeStruct((rows, points), F32),
            jax.ShapeDtypeStruct((2 * cell_rows, LANE), F32),
        ),
        in_specs=[smem] + [hbm] * 8,
        out_specs=(any_space, any_space),
        scratch_shapes=[
            pltpu.SMEM(group_block.shape, jnp.int32),
            pltpu.SMEM(neighbors.shape, jnp.int32),
            vmem(2, rows),
            vmem((2 * ny - 1) * rp, k_all),
            vmem(8 * ny, k_all),
            vmem(chunks, coefs, seg, LANE),
            vmem(chunks, coefs, seg, LANE),
            vmem(k_all, width),
            pltpu.VMEM((m_all, k_all), BF16),
            pltpu.VMEM((m_all, k_all), BF16),
            pltpu.VMEM((far, rp, k_all), BF16),
            pltpu.VMEM((far, rp, k_all), BF16),
            vmem(far, coefs, seg, LANE),
            vmem(far, coefs, seg, LANE),
            vmem(far, 2, rows),
            vmem(chunks, rows, width),
            vmem(far, chunks, rows, width),
            vmem(far, chunks, rows, width),
            vmem(ny, 2 * blocks, LANE),
            vmem(far, 2 * blocks, LANE),
            vmem(nm * 2 * blocks, LANE),
            vmem(2 * groups, LANE),
            pltpu.VMEM((2 * LANE, 2 * groups), BF16),
            pltpu.VMEM((LANE, 2 * groups), BF16),
            vmem(2, LANE, groups),
            vmem(groups, LANE, LANE),
            vmem(2 * cell_rows, LANE),
            vmem(4 * cell_rows, LANE),
            vmem(2, 2 * halo, LANE),
            vmem(2, halo, LANE),
            vmem(cell_rows + 2 * halo, LANE),
            vmem(4, cell_rows, LANE),
            vmem(2 * cell_rows, LANE),
            dma(chunks),
            dma(chunks),
            dma(chunks),
            dma(8),
            dma(far),
            dma(far),
            dma(far),
            dma(far),
            dma(far),
            dma(far),
            dma(far, chunks),
            dma(far, chunks),
            dma(far),
            dma(far),
            dma(max(nm - 1, 1)),
            dma(max(nm - 1, 1)),
            dma(4),
            dma(4),
            dma(chunks),
        ],
        compiler_params=pltpu.CompilerParams(
            collective_id=0, has_side_effects=True, vmem_limit_bytes=40000 * 1024
        ),
        name="adjoint",
    )(group_count, *pinned)
    new_state = state.reshape(cell_rows, 2, LANE).transpose(1, 0, 2)
    return series, new_state.reshape(1, 2, cell_rows * LANE)


def solution(mesh):
    placed = (
        P(None, "freq", "mesh"),
        P(None, "freq"),
        P("mesh", None, None),
        P("mesh"),
        P("mesh"),
        P("freq", None, "mesh"),
        P(None, "mesh"),
        P(None, "mesh"),
    )
    ny = mesh.shape["freq"] // CORES
    return jax.shard_map(
        functools.partial(local, ny, mesh.shape["mesh"]),
        mesh=mesh,
        in_specs=placed,
        out_specs=(P("freq", "mesh"), P("freq", None, "mesh")),
        check_vma=False,
    )
```

profile of v0, /device:TPU:0, one launch (start us, length us, event | category | flops | bytes accessed | tf_op | source)
XLA Modules:
  0.0 52.3 jit_solution(12003983330346108594)
XLA Ops:
  1.3 49.0 %adjoint.1 = (f32[108,4096]{1,0:T(8,128)S(1)}, f32[1024,128]{1,0:T(8,128)S(1)}) custom-call(s32[1]{0:T(128)S(6)} %copy.17.count_smem, s32[128]{0:T(128)} %block_hbm.1, s32[4,512]{1,0:T(4,128)} %neigh_hbm.1, f32[2,108]{1,0:T(2,128)} %tw_hbm.1, f32[4,336,224]{2,1,0:T(8,128)} %constant.2.clone.basis_hbm, f32[54,64,128]{2,1,0:T(8,128)} %bitcast.21, ...), custom_call_target="tpu_custom_call" | custom-call | tf_op jit(solution)/shard_map/adjoint/pallas_call | solution.py:610
  50.3 1.2 %copy.18 = f32[108,4096]{1,0:T(8,128)} copy(f32[108,4096]{1,0:T(8,128)S(1)} %get-tuple-element.8) | data formatting | bytes 3538944
  51.5 0.8 %copy.19 = f32[1,2,65536]{2,1,0:T(2,128)} copy(f32[1,2,65536]{2,1,0:T(2,128)S(1)} %bitcast.20) | data formatting | bytes 1048576
where the time goes:
time: 52.5 us; the launch traced here: 52.3 us
  Pallas kernels  49 us (93%)
  local copies, waits for them, and re-layouts  2.02 us (4%)
  between operations  1.29 us (2%)
    pallas_call x1, Pallas kernels, local(): pl.pallas_call(functools.partial(kernel, (ny, nm, coefs, rows, chunks)),...  49 us
    unnamed x2, local copies, waits for them, and re-layouts  2.02 us

commit v1 on v0

--- a/solution.py
+++ b/solution.py
@@ -43,8 +43,8 @@
     weights_hbm,
     wave_hbm,
     coup_hbm,
-    series_hbm,
-    state_hbm,
+    series,
+    state,
     block_smem,
     neigh_smem,
     tw_own,
@@ -60,7 +60,6 @@
     raw,
     raw_peer,
     tw_all,
-    own,
     outgoing,
     incoming,
     part,
@@ -77,7 +76,6 @@
     halo2,
     ext,
     gathered,
-    state,
     spec_sem,
     swap_send,
     swap_recv,
@@ -96,7 +94,6 @@
     wall_recv,
     halo_send,
     halo_recv,
-    out_sem,
 ):
     ny, nm, coefs, rows, chunks = dims
     groups = weights.shape[0]
@@ -217,10 +214,8 @@
             peer(-1 if side else 1),
         )
 
-    def store_series(c):
-        return pltpu.make_async_copy(
-            own.at[c], series_hbm.at[:, pl.ds(pl.multiple_of(c * width, width), width)], out_sem.at[c]
-        )
+    def columns(c):
+        return pl.ds(pl.multiple_of(c * width, width), width)
 
     load_wave = pltpu.make_async_copy(wave_hbm, wave, load_sem.at[0])
     load_coup = pltpu.make_async_copy(coup_hbm, coup, load_sem.at[1])
@@ -299,7 +294,7 @@
         return dot(high, s_high) + dot(lhs_low[first:last, :], s_high) + dot(high, s_low)
 
     def keep_series(c, total):
-        own[c] = total[0:rows]
+        series[:, columns(c)] = total[0:rows]
         for d in range(1, ny):
             outgoing[d - 1, c] = total[d * rp : d * rp + rows]
 
@@ -421,7 +416,7 @@
 
     lax.fori_loop(0, cell_rows // wave_rows, first_step, 0)
 
-    total = own[chunks - 1]
+    total = series[:, columns(chunks - 1)]
     for d in range(1, ny):
         high, low = split(basis_own[m1 + (d - 1) * rp : m1 + d * rp, :])
         cross_high[d - 1] = high
@@ -431,8 +426,7 @@
         high = cross_high[d - 1]
         product_d = dot(high, s_high) + dot(cross_low[d - 1], s_high) + dot(high, s_low)
         total += product_d[0:rows]
-    own[chunks - 1] = total
-    store_series(chunks - 1).start()
+    series[:, columns(chunks - 1)] = total
 
     for o in range(1, nm):
         send_wall(o).wait_recv()
@@ -505,16 +499,13 @@
     lax.fori_loop(0, cell_rows // wave_rows, second_step, 0)
     bottom = pl.ds(1, groups, stride=2)
     state[bottom, :] = state[bottom, :] + push[1]
-    store_state = pltpu.make_async_copy(state, state_hbm, load_sem.at[3])
-    store_state.start()
 
     def finish(c, carry):
-        total = own[c]
+        total = series[:, columns(c)]
         for d in range(1, ny):
             send_series(d, c).wait_recv()
             total += incoming[d - 1, c]
-        own[c] = total
-        store_series(c).start()
+        series[:, columns(c)] = total
         return carry
 
     lax.fori_loop(0, chunks - 1, finish, 0)
@@ -523,12 +514,10 @@
         swap(c).wait_send()
         for d in range(1, ny):
             send_series(d, c).wait_send()
-        store_series(c).wait()
         return carry
 
     lax.fori_loop(0, chunks - 1, drain, 0)
     swap(chunks - 1).wait_send()
-    store_series(chunks - 1).wait()
     for d in range(1, ny):
         send_raw(d).wait_send()
         pass_raw(d).wait_send()
@@ -539,7 +528,17 @@
     for side in range(2):
         send_halo1(side).wait_send()
         send_halo2(side).wait_send()
-    store_state.wait()
+
+
+def store(series, state, series_hbm, state_hbm, sem):
+    copies = [
+        pltpu.make_async_copy(series, series_hbm, sem.at[0]),
+        pltpu.make_async_copy(state, state_hbm, sem.at[1]),
+    ]
+    for copy in copies:
+        copy.start()
+    for copy in copies:
+        copy.wait()
 
 
 def chip_basis(ny, coefs, rows, horizon):
@@ -592,7 +591,7 @@
     dma = lambda *shape: pltpu.SemaphoreType.DMA(shape)
     smem = pl.BlockSpec(memory_space=pltpu.SMEM)
     hbm = pl.BlockSpec(memory_space=pltpu.HBM)
-    any_space = pl.BlockSpec(memory_space=pl.ANY)
+    on_chip = pl.BlockSpec(memory_space=pltpu.VMEM)
     far = max(ny - 1, 1)
     pinned = [
         pltpu.with_memory_space_constraint(x, pltpu.HBM)
@@ -607,14 +606,15 @@
             coup,
         )
     ]
+    outs = (
+        jax.ShapeDtypeStruct((rows, points), F32),
+        jax.ShapeDtypeStruct((2 * cell_rows, LANE), F32),
+    )
     series, state = pl.pallas_call(
         functools.partial(kernel, (ny, nm, coefs, rows, chunks)),
-        out_shape=(
-            jax.ShapeDtypeStruct((rows, points), F32),
-            jax.ShapeDtypeStruct((2 * cell_rows, LANE), F32),
-        ),
+        out_shape=outs,
         in_specs=[smem] + [hbm] * 8,
-        out_specs=(any_space, any_space),
+        out_specs=(on_chip, on_chip),
         scratch_shapes=[
             pltpu.SMEM(group_block.shape, jnp.int32),
             pltpu.SMEM(neighbors.shape, jnp.int32),
@@ -631,7 +631,6 @@
             vmem(far, coefs, seg, LANE),
             vmem(far, coefs, seg, LANE),
             vmem(far, 2, rows),
-            vmem(chunks, rows, width),
             vmem(far, chunks, rows, width),
             vmem(far, chunks, rows, width),
             vmem(ny, 2 * blocks, LANE),
@@ -648,7 +647,6 @@
             vmem(2, halo, LANE),
             vmem(cell_rows + 2 * halo, LANE),
             vmem(4, cell_rows, LANE),
-            vmem(2 * cell_rows, LANE),
             dma(chunks),
             dma(chunks),
             dma(chunks),
@@ -667,13 +665,21 @@
             dma(max(nm - 1, 1)),
             dma(4),
             dma(4),
-            dma(chunks),
         ],
         compiler_params=pltpu.CompilerParams(
             collective_id=0, has_side_effects=True, vmem_limit_bytes=40000 * 1024
         ),
         name="adjoint",
     )(group_count, *pinned)
+    series, state = pl.pallas_call(
+        store,
+        out_shape=outs,
+        in_specs=[pl.BlockSpec(memory_space=pl.ANY)] * 2,
+        out_specs=(hbm, hbm),
+        scratch_shapes=[dma(2)],
+        compiler_params=pltpu.CompilerParams(vmem_limit_bytes=1024 * 1024),
+        name="store",
+    )(series, state)
     new_state = state.reshape(cell_rows, 2, LANE).transpose(1, 0, 2)
     return series, new_state.reshape(1, 2, cell_rows * LANE)
 

time: 52.5 us -> 51.7 us (0.985)
  local copies, waits for them, and re-layouts: 2.02 us -> 0 us
  Pallas kernels: 49 us -> 50.3 us
    unnamed x2 -> x0, local copies, waits for them, and re-layouts: 2.02 us -> none
    pallas_call x0 -> x1, Pallas kernels: none -> 1.42 us  [local(): pl.pallas_call(store, out_shape=outs, in_specs=[pl.BlockSpec(memory_space...]
where the time goes in v1:
time: 51.7 us; the launch traced here: 51.6 us
  Pallas kernels  50.3 us (97%)
  between operations  1.29 us (2%)
    pallas_call x1, Pallas kernels, local(): pl.pallas_call(functools.partial(kernel, (ny, nm, coefs, rows, chunks)),...  48.9 us
    pallas_call x1, Pallas kernels, local(): pl.pallas_call(store, out_shape=outs, in_specs=[pl.BlockSpec(memory_space...  1.42 us

profile of v1, /device:TPU:0, one launch (start us, length us, event | category | flops | bytes accessed | tf_op | source)
XLA Modules:
  0.0 51.6 jit_solution(3684947393771368260)
XLA Ops:
  1.3 48.9 %adjoint.1 = (f32[108,4096]{1,0:T(8,128)S(1)}, f32[1024,128]{1,0:T(8,128)S(1)}) custom-call(s32[1]{0:T(128)S(6)} %copy.15.count_smem, s32[128]{0:T(128)} %block_hbm.1, s32[4,512]{1,0:T(4,128)} %neigh_hbm.1, f32[2,108]{1,0:T(2,128)} %tw_hbm.1, f32[4,336,224]{2,1,0:T(8,128)} %constant.2.clone.basis_hbm, f32[54,64,128]{2,1,0:T(8,128)} %bitcast.20, ...), custom_call_target="tpu_custom_call" | custom-call | tf_op jit(solution)/shard_map/adjoint/pallas_call | solution.py:613
  50.1 1.4 %store.1 = (f32[108,4096]{1,0:T(8,128)}, f32[1024,128]{1,0:T(8,128)}) custom-call(f32[108,4096]{1,0:T(8,128)S(1)} %get-tuple-element.6.series, f32[1024,128]{1,0:T(8,128)S(1)} %get-tuple-element.7.state), custom_call_target="tpu_custom_call" | custom-call | tf_op jit(solution)/shard_map/store/pallas_call | solution.py:674

commit v2 on v1

--- a/solution.py
+++ b/solution.py
@@ -94,6 +94,10 @@
     wall_recv,
     halo_send,
     halo_recv,
+    go,
+    seen,
+    peers_in,
+    all_in,
 ):
     ny, nm, coefs, rows, chunks = dims
     groups = weights.shape[0]
@@ -148,7 +152,7 @@
 
     def send_raw(d):
         return remote(
-            spec_hbm.at[:, pl.ds((chunks - 1) * seg, seg), :],
+            own_spec.at[chunks - 1],
             raw.at[d - 1],
             raw_send.at[d - 1],
             raw_recv.at[d - 1],
@@ -214,6 +218,13 @@
             peer(-1 if side else 1),
         )
 
+    inside = (me > 0, me < nm - 1)
+
+    def halo_each(copy, method):
+        for side in range(2):
+            there = inside[side] if method == "wait_recv" else inside[1 - side]
+            pl.when(there)(getattr(copy(side), method))
+
     def columns(c):
         return pl.ds(pl.multiple_of(c * width, width), width)
 
@@ -228,34 +239,79 @@
 
     load_tw.start()
     load_basis.start()
-    for c in range(chunks):
+    for c in (chunks - 1, *range(chunks - 1)):
         load_spec(c).start()
     load_wave.start()
     load_neigh.start()
     load_block.start()
 
     barrier = pltpu.get_barrier_semaphore()
-    pl.semaphore_signal(
-        barrier, inc=1, device_id={"freq": partner}, device_id_type=pl.DeviceIdType.MESH
-    )
-    for d in range(1, ny):
+    first_core, first_chip = core == 0, chip == 0
+    other_core, other_chip = core == 1, chip != 0
+
+    def signal(sem, axis, target):
         pl.semaphore_signal(
-            barrier, inc=1, device_id={"freq": at_chip(d)}, device_id_type=pl.DeviceIdType.MESH
-        )
-    for o in range(1, nm):
-        pl.semaphore_signal(
-            barrier, inc=1, device_id={"mesh": peer(o)}, device_id_type=pl.DeviceIdType.MESH
-        )
-    pl.semaphore_wait(barrier, 1 + (ny - 1) + (nm - 1))
-
-    swap(0).start()
+            sem, inc=1, device_id={axis: target}, device_id_type=pl.DeviceIdType.MESH
+        )
+
+    @pl.when(first_core)
+    def _():
+        for d in range(1, ny):
+            signal(barrier, "freq", at_chip(d))
+
+    @pl.when(first_core == other_chip)
+    def _():
+        signal(barrier, "freq", partner)
+
+    @pl.when(first_core & first_chip)
+    def _():
+        pl.semaphore_wait(barrier, ny)
+        signal(go, "freq", partner)
+
+    @pl.when(first_core & other_chip)
+    def _():
+        pl.semaphore_wait(barrier, ny - 1)
+
+    @pl.when(other_core & other_chip)
+    def _():
+        pl.semaphore_wait(barrier, 1)
+        signal(go, "freq", partner)
+
     load_tw.wait()
-    for d in range(1, ny):
-        send_tw(d).start()
-    for d in range(1, ny):
-        send_raw(d).start()
-    for c in range(1, chunks):
+    load_spec(chunks - 1).wait()
+
+    def send_first():
+        for d in range(1, ny):
+            send_tw(d).start()
+            send_raw(d).start()
+
+    pl.when(first_core)(send_first)
+
+    @pl.when(first_core == other_chip)
+    def _():
+        pl.semaphore_wait(go, 1)
+
+    for c in range(chunks):
         swap(c).start()
+
+    @pl.when(first_core)
+    def _():
+        for d in range(1, ny):
+            signal(seen.at[d - 1], "freq", at_chip(d))
+        for d in range(1, ny):
+            pl.semaphore_wait(seen.at[d - 1], 1)
+        signal(peers_in, "freq", partner)
+
+    @pl.when(other_core)
+    def _():
+        pl.semaphore_wait(peers_in, 1)
+        send_first()
+
+    @pl.when(other_core & first_chip)
+    def _():
+        for o in range(1, nm):
+            signal(barrier, "mesh", peer(o))
+
     load_coup.start()
     load_weights.start()
 
@@ -265,9 +321,6 @@
     high, low = split(basis_own[0:m1, :])
     lhs_high[0:m1, :] = high
     lhs_low[0:m1, :] = low
-    load_wave.wait()
-    for side in range(2):
-        send_halo1(side).start()
 
     own_rows = own_spec.reshape(chunks * coefs * seg, LANE)
     peer_rows = peer_spec.reshape(chunks * coefs * seg, LANE)
@@ -285,7 +338,10 @@
         return split(staged[...])
 
     def stage_chunk(c):
-        load_spec(c).wait()
+        @pl.when(c < chunks - 1)
+        def _():
+            load_spec(c).wait()
+
         swap(c).wait_recv()
         return stage((own_rows, peer_rows), c)
 
@@ -350,6 +406,21 @@
         return carry
 
     lax.fori_loop(EARLY, chunks - 1, later, 0)
+
+    @pl.when(other_core & first_chip)
+    def _():
+        pl.semaphore_wait(barrier, nm - 1)
+        for d in range(ny):
+            signal(all_in, "freq", d * CORES)
+            if d:
+                signal(all_in, "freq", d * CORES + 1)
+
+    @pl.when(first_core | other_chip)
+    def _():
+        pl.semaphore_wait(all_in, 1)
+
+    load_wave.wait()
+    halo_each(send_halo1, "start")
     for d in range(1, ny):
         send_raw(d).wait_recv()
         pass_raw(d).start()
@@ -386,8 +457,7 @@
     inside_low = (jnp.zeros((halo, LANE), jnp.int32) + me) > 0
     inside_high = (jnp.zeros((halo, LANE), jnp.int32) + me) < nm - 1
 
-    for side in range(2):
-        send_halo1(side).wait_recv()
+    halo_each(send_halo1, "wait_recv")
     ext[0:halo, :] = jnp.where(inside_low, halo1[0, pl.ds(1, halo, stride=2), :], 0.0)
     ext[halo + cell_rows :, :] = jnp.where(
         inside_high, halo1[1, pl.ds(1, halo, stride=2), :], 0.0
@@ -479,10 +549,8 @@
         return carry
 
     lax.fori_loop(0, cell_rows // wave_rows, stage_stepped, 0)
-    for side in range(2):
-        send_halo2(side).start()
-    for side in range(2):
-        send_halo2(side).wait_recv()
+    halo_each(send_halo2, "start")
+    halo_each(send_halo2, "wait_recv")
     ext[0:halo, :] = jnp.where(inside_low, halo2[0], 0.0)
     ext[halo + cell_rows :, :] = jnp.where(inside_high, halo2[1], 0.0)
     gather()
@@ -525,9 +593,8 @@
         send_part(d).wait_send()
     for o in range(1, nm):
         send_wall(o).wait_send()
-    for side in range(2):
-        send_halo1(side).wait_send()
-        send_halo2(side).wait_send()
+    halo_each(send_halo1, "wait_send")
+    halo_each(send_halo2, "wait_send")
 
 
 def store(series, state, series_hbm, state_hbm, sem):
@@ -665,6 +732,10 @@
             dma(max(nm - 1, 1)),
             dma(4),
             dma(4),
+            pltpu.SemaphoreType.REGULAR,
+            pltpu.SemaphoreType.REGULAR((far,)),
+            pltpu.SemaphoreType.REGULAR,
+            pltpu.SemaphoreType.REGULAR,
         ],
         compiler_params=pltpu.CompilerParams(
             collective_id=0, has_side_effects=True, vmem_limit_bytes=40000 * 1024

time: 51.7 us -> 48.4 us (0.936)
  Pallas kernels: 50.3 us -> 46.8 us
    pallas_call x1, Pallas kernels: 48.9 us -> 45.4 us  [local(): pl.pallas_call(functools.partial(kernel, (ny, nm, coefs, rows, chunks)),...]
where the time goes in v2:
time: 48.4 us; the launch traced here: 48.1 us
  Pallas kernels  46.8 us (97%)
  between operations  1.29 us (3%)
    pallas_call x1, Pallas kernels, local(): pl.pallas_call(functools.partial(kernel, (ny, nm, coefs, rows, chunks)),...  45.4 us
    pallas_call x1, Pallas kernels, local(): pl.pallas_call(store, out_shape=outs, in_specs=[pl.BlockSpec(memory_space...  1.42 us

profile of v2, /device:TPU:0, one launch (start us, length us, event | category | flops | bytes accessed | tf_op | source)
XLA Modules:
  0.0 48.1 jit_solution(8037686124659845229)
XLA Ops:
  1.3 45.4 %adjoint.1 = (f32[108,4096]{1,0:T(8,128)S(1)}, f32[1024,128]{1,0:T(8,128)S(1)}) custom-call(s32[1]{0:T(128)S(6)} %copy.15.count_smem, s32[128]{0:T(128)} %block_hbm.1, s32[4,512]{1,0:T(4,128)} %neigh_hbm.1, f32[2,108]{1,0:T(2,128)} %tw_hbm.1, f32[4,336,224]{2,1,0:T(8,128)} %constant.2.clone.basis_hbm, f32[54,64,128]{2,1,0:T(8,128)} %bitcast.20, ...), custom_call_target="tpu_custom_call" | custom-call | tf_op jit(solution)/shard_map/adjoint/pallas_call | solution.py:680
  46.7 1.4 %store.1 = (f32[108,4096]{1,0:T(8,128)}, f32[1024,128]{1,0:T(8,128)}) custom-call(f32[108,4096]{1,0:T(8,128)S(1)} %get-tuple-element.6.series, f32[1024,128]{1,0:T(8,128)S(1)} %get-tuple-element.7.state), custom_call_target="tpu_custom_call" | custom-call | tf_op jit(solution)/shard_map/store/pallas_call | solution.py:745

commit v3 on v2

--- a/solution.py
+++ b/solution.py
@@ -13,14 +13,15 @@
 CORES = 2
 HALO_CELLS = 4096
 BLOCKS_PER_CHUNK = 4
-EARLY = 2
+RAW = 2
+PAIR = 2
 HIGHEST = lax.Precision.HIGHEST
 F32 = jnp.float32
 BF16 = jnp.bfloat16
 
 
-def pad8(n):
-    return (n + 7) // 8 * 8
+def pad(n, to):
+    return (n + to - 1) // to * to
 
 
 def split(x):
@@ -66,10 +67,10 @@
     part_in,
     wall,
     picked,
-    xt_high,
-    xt_low,
+    asked,
     turned,
     weights,
+    lined,
     wave,
     coup,
     halo1,
@@ -101,13 +102,17 @@
 ):
     ny, nm, coefs, rows, chunks = dims
     groups = weights.shape[0]
-    kp, rp = pad8(coefs), pad8(rows)
+    kp, rp, fb = pad(coefs, 8), pad(rows, 8), pad(rows, 16)
+    rb = fb + 16
     m1 = ny * rp
-    per = part.shape[1] // 2
+    per = part.shape[2]
     cell_rows = ext.shape[0] - 2 * halo1.shape[1] // 2
     halo = halo1.shape[1] // 2
     width = BLOCKS_PER_CHUNK * LANE
     seg = 2 * BLOCKS_PER_CHUNK
+    summed = chunks - RAW
+    whole_rows = rows // 8 * 8
+    rest = rows - whole_rows
 
     freq = lax.axis_index("freq")
     me = lax.axis_index("mesh")
@@ -132,18 +137,28 @@
 
     def load_spec(c):
         return pltpu.make_async_copy(
-            spec_hbm.at[:, pl.ds(c * seg, seg), :], own_spec.at[c], spec_sem.at[c]
-        )
+            spec_hbm.at[:, pl.ds(c * seg, seg), :],
+            own_spec.at[c],
+            spec_sem.at[1 if c >= summed else 0],
+        )
+
+    def loaded(first, count, sem):
+        span = own_spec.at[pl.ds(first, count)]
+        return pltpu.make_async_copy(span, span, spec_sem.at[sem])
 
     def swap(c):
         return remote(
             spec_hbm.at[:, pl.ds(c * seg, seg), :],
             peer_spec.at[c],
-            swap_send.at[c],
-            swap_recv.at[c],
+            swap_send.at[0],
+            swap_recv.at[c // PAIR],
             "freq",
             partner,
         )
+
+    def swapped(first, count):
+        span = peer_spec.at[pl.ds(first, count)]
+        return remote(span, span, swap_send.at[0], swap_recv.at[first // PAIR], "freq", partner)
 
     def send_tw(d):
         return remote(
@@ -152,7 +167,7 @@
 
     def send_raw(d):
         return remote(
-            own_spec.at[chunks - 1],
+            own_spec.at[pl.ds(summed, RAW)],
             raw.at[d - 1],
             raw_send.at[d - 1],
             raw_recv.at[d - 1],
@@ -170,19 +185,20 @@
             partner,
         )
 
-    def send_series(d, c):
+    def send_series(d, first, count):
+        span = pl.ds(first, count)
         return remote(
-            outgoing.at[d - 1, c],
-            incoming.at[d - 1, c],
-            ser_send.at[d - 1, c],
-            ser_recv.at[d - 1, c],
+            outgoing.at[d - 1, span],
+            incoming.at[d - 1, span],
+            ser_send.at[d - 1],
+            ser_recv.at[d - 1, jnp.where(first == summed - 1, 1, 0)],
             "freq",
             at_chip(d),
         )
 
     def send_part(d):
         return remote(
-            part.at[d],
+            part.at[d, :, pl.ds(0, summed * BLOCKS_PER_CHUNK), :],
             part_in.at[d - 1],
             part_send.at[d - 1],
             part_recv.at[d - 1],
@@ -191,10 +207,12 @@
         )
 
     def send_wall(o):
-        mine = pl.ds(pl.multiple_of(me * 2 * per, 8), 2 * per)
-        return remote(
-            wall.at[mine], wall.at[mine], wall_send.at[o - 1], wall_recv.at[o - 1], "mesh", peer(o)
-        )
+        mine = wall.at[:, pl.ds(pl.multiple_of(me * per, 8), per), :]
+        return remote(mine, mine, wall_send.at[0], wall_recv.at[0], "mesh", peer(o))
+
+    def walled():
+        span = wall.at[:, pl.ds(0, (nm - 1) * per), :]
+        return remote(span, span, wall_send.at[0], wall_recv.at[0], "mesh", peer(1))
 
     def send_halo1(side):
         first = 0 if side else 2 * (cell_rows - halo)
@@ -230,17 +248,18 @@
 
     load_wave = pltpu.make_async_copy(wave_hbm, wave, load_sem.at[0])
     load_coup = pltpu.make_async_copy(coup_hbm, coup, load_sem.at[1])
-    load_weights = pltpu.make_async_copy(weights_hbm, weights, load_sem.at[2])
-
-    load_tw = pltpu.make_async_copy(tw_hbm, tw_own, load_sem.at[4])
-    load_basis = pltpu.make_async_copy(basis_hbm.at[freq], basis_own, load_sem.at[5])
-    load_neigh = pltpu.make_async_copy(neigh_hbm, neigh_smem, load_sem.at[6])
-    load_block = pltpu.make_async_copy(block_hbm, block_smem, load_sem.at[7])
+    load_weights = pltpu.make_async_copy(
+        weights_hbm, weights.at[:, pl.ds(0, LANE), :], load_sem.at[2]
+    )
+    load_tw = pltpu.make_async_copy(tw_hbm, tw_own, load_sem.at[3])
+    load_basis = pltpu.make_async_copy(basis_hbm.at[freq], basis_own, load_sem.at[4])
+    load_neigh = pltpu.make_async_copy(neigh_hbm, neigh_smem, load_sem.at[5])
+    load_block = pltpu.make_async_copy(block_hbm, block_smem, load_sem.at[6])
 
     load_tw.start()
+    for c in (*range(summed, chunks), *range(summed)):
+        load_spec(c).start()
     load_basis.start()
-    for c in (chunks - 1, *range(chunks - 1)):
-        load_spec(c).start()
     load_wave.start()
     load_neigh.start()
     load_block.start()
@@ -278,7 +297,7 @@
         signal(go, "freq", partner)
 
     load_tw.wait()
-    load_spec(chunks - 1).wait()
+    loaded(summed, RAW, 1).wait()
 
     def send_first():
         for d in range(1, ny):
@@ -318,15 +337,36 @@
     staged[...] = jnp.zeros_like(staged)
     folded[...] = jnp.zeros_like(folded)
     load_basis.wait()
-    high, low = split(basis_own[0:m1, :])
-    lhs_high[0:m1, :] = high
-    lhs_low[0:m1, :] = low
+    for d in range(ny):
+        high, low = split(basis_own[d * rp : (d + 1) * rp, :])
+        lhs_high[d * rb : d * rb + rp, :] = high
+        lhs_low[d * rb : d * rb + rp, :] = low
+    for d in range(1, ny):
+        high, low = split(basis_own[m1 + (d - 1) * rp : m1 + d * rp, :])
+        cross_high[d - 1, 0:rp, :] = high
+        cross_low[d - 1, 0:rp, :] = low
+    for d in range(2 * ny - 1):
+        if 0 < d < ny:
+            send_tw(d).wait_recv()
+        folded[16 * d : 16 * d + 2, :] = jnp.dot(
+            tw_all[d - 1] if 0 < d < ny else tw_own[...],
+            basis_own[d * rp : d * rp + rows, :],
+            precision=HIGHEST,
+            preferred_element_type=F32,
+        )
+        high, low = split(folded[16 * d : 16 * (d + 1), :])
+        if d < ny:
+            lhs_high[d * rb + fb : (d + 1) * rb, :] = high
+            lhs_low[d * rb + fb : (d + 1) * rb, :] = low
+        else:
+            cross_high[d - ny, fb:rb, :] = high
+            cross_low[d - ny, fb:rb, :] = low
 
     own_rows = own_spec.reshape(chunks * coefs * seg, LANE)
     peer_rows = peer_spec.reshape(chunks * coefs * seg, LANE)
-
-    raw_rows = raw.reshape(max(ny - 1, 1) * coefs * seg, LANE)
-    raw_peer_rows = raw_peer.reshape(max(ny - 1, 1) * coefs * seg, LANE)
+    far = max(ny - 1, 1)
+    raw_rows = raw.reshape(far * RAW * coefs * seg, LANE)
+    raw_peer_rows = raw_peer.reshape(far * RAW * coefs * seg, LANE)
 
     def stage(sources, c):
         for p, source in enumerate(sources):
@@ -337,75 +377,66 @@
                     staged[base : base + coefs, j * LANE : (j + 1) * LANE] = piece
         return split(staged[...])
 
-    def stage_chunk(c):
-        @pl.when(c < chunks - 1)
+    def product(high, low, s_high, s_low):
+        return dot(high, s_high) + dot(low, s_high) + dot(high, s_low)
+
+    def keep_part(c, total, d):
+        for s in range(2):
+            row = d * rb + fb + s
+            for j in range(BLOCKS_PER_CHUNK):
+                part[d, s, pl.ds(c * BLOCKS_PER_CHUNK + j, 1), :] = total[
+                    row : row + 1, j * LANE : (j + 1) * LANE
+                ]
+
+    def pieces(c):
+        for j in range(BLOCKS_PER_CHUNK):
+            lanes = pl.ds(pl.multiple_of(c * width + j * LANE, LANE), LANE)
+            yield j, slice(0, whole_rows), slice(j * whole_rows, (j + 1) * whole_rows), lanes
+            if rest:
+                first = BLOCKS_PER_CHUNK * whole_rows + j * rest
+                yield j, slice(whole_rows, rows), slice(first, first + rest), lanes
+
+    def summed_chunk(c, carry):
+        @pl.when(c % PAIR == 0)
         def _():
-            load_spec(c).wait()
-
-        swap(c).wait_recv()
-        return stage((own_rows, peer_rows), c)
-
-    def product(first, last, s_high, s_low):
-        high = lhs_high[first:last, :]
-        return dot(high, s_high) + dot(lhs_low[first:last, :], s_high) + dot(high, s_low)
-
-    def keep_series(c, total):
+            swapped(c, PAIR).wait_recv()
+
+        s_high, s_low = stage((own_rows, peer_rows), c)
+        total = product(lhs_high[...], lhs_low[...], s_high, s_low)
         series[:, columns(c)] = total[0:rows]
+        keep_part(c, total, 0)
         for d in range(1, ny):
-            outgoing[d - 1, c] = total[d * rp : d * rp + rows]
-
-    def keep_part(c, total):
-        for d in range(ny):
-            for s in range(2):
-                row = 8 * d + s
-                for j in range(BLOCKS_PER_CHUNK):
-                    part[d, pl.ds(s * per + c * BLOCKS_PER_CHUNK + j, 1), :] = total[
-                        row : row + 1, j * LANE : (j + 1) * LANE
-                    ]
-
-    m_all = m1 + 8 * ny
-    s_high, s_low = stage_chunk(0)
-    keep_series(0, product(0, m1, s_high, s_low))
-    for d in range(1, ny):
-        send_series(d, 0).start()
-    for d in range(ny):
-        if d:
-            send_tw(d).wait_recv()
-        tw = tw_all[d - 1] if d else tw_own[...]
-        folded[8 * d : 8 * d + 2, :] = jnp.dot(
-            tw,
-            basis_own[d * rp : d * rp + rows, :],
-            precision=HIGHEST,
-            preferred_element_type=F32,
-        )
-    high, low = split(folded[...])
-    lhs_high[m1:, :] = high
-    lhs_low[m1:, :] = low
-    keep_part(0, product(m1, m_all, s_high, s_low))
-
-    def partial_chunk(c, carry):
-        s_high, s_low = stage_chunk(c)
-        total = product(0, m_all, s_high, s_low)
-        keep_series(c, total)
-        keep_part(c, total[m1:])
-
-        @pl.when(c < EARLY)
-        def _():
-            for d in range(1, ny):
-                send_series(d, c).start()
-
-        return carry
-
-    lax.fori_loop(1, chunks, partial_chunk, 0)
+            keep_part(c, total, d)
+            for j, take, put, _ in pieces(c):
+                outgoing[d - 1, c, put, :] = total[
+                    d * rb + take.start : d * rb + take.stop, j * LANE : (j + 1) * LANE
+                ]
+        return carry
+
+    loaded(0, summed, 0).wait()
+    lax.fori_loop(0, summed, summed_chunk, 0)
     for d in range(1, ny):
         send_part(d).start()
 
-    def later(c, carry):
+    def send_chunk(c, carry):
         for d in range(1, ny):
-            send_series(d, c).start()
-        return carry
-
-    lax.fori_loop(EARLY, chunks - 1, later, 0)
+            send_series(d, c, 1).start()
+        return carry
+
+    lax.fori_loop(0, summed, send_chunk, 0)
+
+    def raw_chunk(c, carry):
+        @pl.when(c % PAIR == 0)
+        def _():
+            swapped(c, PAIR).wait_recv()
+
+        s_high, s_low = stage((own_rows, peer_rows), c)
+        total = product(lhs_high[0:rb, :], lhs_low[0:rb, :], s_high, s_low)
+        series[:, columns(c)] = total[0:rows]
+        keep_part(c, total, 0)
+        return carry
+
+    lax.fori_loop(summed, chunks, raw_chunk, 0)
 
     @pl.when(other_core & first_chip)
     def _():
@@ -421,6 +452,21 @@
 
     load_wave.wait()
     halo_each(send_halo1, "start")
+
+    pitch = weights.shape[1]
+    weight_rows = weights.reshape(groups * pitch, LANE)
+    load_weights.wait()
+
+    def line_up(t, carry):
+        for i in range(4):
+            f = t * 4 + i
+            lined[pl.ds(pl.multiple_of(f * LANE, LANE), LANE), :] = weight_rows[
+                pl.ds(f, groups, stride=pitch), :
+            ].T
+        return carry
+
+    lax.fori_loop(0, LANE // 4, line_up, 0)
+
     for d in range(1, ny):
         send_raw(d).wait_recv()
         pass_raw(d).start()
@@ -463,16 +509,6 @@
         inside_high, halo1[1, pl.ds(1, halo, stride=2), :], 0.0
     )
     load_coup.wait()
-
-    for d in range(1, ny):
-        send_part(d).wait_recv()
-    weighted = part[0]
-    for d in range(1, ny):
-        weighted += part_in[d - 1]
-    wall[pl.ds(pl.multiple_of(me * 2 * per, 8), 2 * per), :] = weighted
-    for o in range(1, nm):
-        send_wall(o).start()
-
     gather()
 
     def first_step(b, carry):
@@ -486,57 +522,62 @@
 
     lax.fori_loop(0, cell_rows // wave_rows, first_step, 0)
 
-    total = series[:, columns(chunks - 1)]
     for d in range(1, ny):
-        high, low = split(basis_own[m1 + (d - 1) * rp : m1 + d * rp, :])
-        cross_high[d - 1] = high
-        cross_low[d - 1] = low
         pass_raw(d).wait_recv()
-        s_high, s_low = stage((raw_rows, raw_peer_rows), d - 1)
-        high = cross_high[d - 1]
-        product_d = dot(high, s_high) + dot(cross_low[d - 1], s_high) + dot(high, s_low)
-        total += product_d[0:rows]
-    series[:, columns(chunks - 1)] = total
-
+    for r in range(RAW):
+        c = summed + r
+        total = series[:, columns(c)]
+        extra = None
+        for d in range(1, ny):
+            s_high, s_low = stage((raw_rows, raw_peer_rows), (d - 1) * RAW + r)
+            cross = product(cross_high[d - 1], cross_low[d - 1], s_high, s_low)
+            total += cross[0:rows]
+            extra = cross[fb : fb + 2] if extra is None else extra + cross[fb : fb + 2]
+        series[:, columns(c)] = total
+        if extra is not None:
+            for s in range(2):
+                for j in range(BLOCKS_PER_CHUNK):
+                    at = pl.ds(c * BLOCKS_PER_CHUNK + j, 1)
+                    part[0, s, at, :] = (
+                        part[0, s, at, :] + extra[s : s + 1, j * LANE : (j + 1) * LANE]
+                    )
+
+    for d in range(1, ny):
+        send_part(d).wait_recv()
+    first_blocks = summed * BLOCKS_PER_CHUNK
+    base = pl.multiple_of(me * per, 8)
+    for s in range(2):
+        weighted = part[0, s, 0:first_blocks, :]
+        for d in range(1, ny):
+            weighted += part_in[d - 1, s]
+        wall[s, pl.ds(base, first_blocks), :] = weighted
+        wall[s, pl.ds(base + first_blocks, per - first_blocks), :] = part[0, s, first_blocks:, :]
     for o in range(1, nm):
-        send_wall(o).wait_recv()
+        send_wall(o).start()
+    walled().wait_recv()
 
     def pick(t, carry):
         for i in range(8):
             g = t * 8 + i
             block = block_smem[g]
-            row = (block // per) * (2 * per) + block % per
-            picked[pl.ds(g, 1), :] = wall[pl.ds(row, 1), :]
-            picked[pl.ds(groups + g, 1), :] = wall[pl.ds(row + per, 1), :]
+            for s in range(2):
+                picked[s, pl.ds(g, 1), :] = wall[s, pl.ds(block, 1), :]
         return carry
 
     lax.fori_loop(0, groups // 8, pick, 0)
-    high, low = split(picked[...].T)
-    xt_high[0:LANE, :] = high
-    xt_high[LANE:, :] = high
-    xt_low[...] = low
-    load_weights.wait()
-    batch = 8
-    lane = lax.broadcasted_iota(jnp.int32, (LANE, groups), 1)
+    for s in range(2):
+        asked[s] = picked[s].T
 
     def interpolate(t, carry):
-        block = weights[pl.ds(t * batch, batch)].reshape(batch * LANE, LANE)
-        w_high, w_low = split(block)
-        both = jnp.concatenate([w_high, w_low], axis=1)
-        result = dot(both, xt_high[...]) + dot(w_high, xt_low[...])
+        faces = lined[pl.ds(pl.multiple_of(t * 8 * LANE, 8 * LANE), 8 * LANE), :]
+        faces = faces.reshape(8, LANE, groups)
         for s in range(2):
-            column = turned[s]
-            for i in range(batch):
-                column = jnp.where(
-                    lane == t * batch + i,
-                    result[i * LANE : (i + 1) * LANE, s * groups : (s + 1) * groups],
-                    column,
-                )
-            turned[s] = column
-        return carry
-
-    turned[...] = jnp.zeros_like(turned)
-    lax.fori_loop(0, groups // batch, interpolate, 0)
+            turned[s, pl.ds(pl.multiple_of(t * 8, 8), 8), :] = jnp.sum(
+                faces * asked[s][None], axis=1
+            )
+        return carry
+
+    lax.fori_loop(0, LANE // 8, interpolate, 0)
     alive = lax.broadcasted_iota(jnp.int32, (groups, LANE), 0) < count_smem[0]
     push = [jnp.where(alive, turned[s].T, 0.0) for s in range(2)]
 
@@ -568,33 +609,30 @@
     bottom = pl.ds(1, groups, stride=2)
     state[bottom, :] = state[bottom, :] + push[1]
 
-    def finish(c, carry):
-        total = series[:, columns(c)]
-        for d in range(1, ny):
-            send_series(d, c).wait_recv()
-            total += incoming[d - 1, c]
-        series[:, columns(c)] = total
-        return carry
-
-    lax.fori_loop(0, chunks - 1, finish, 0)
-
-    def drain(c, carry):
-        swap(c).wait_send()
-        for d in range(1, ny):
-            send_series(d, c).wait_send()
-        return carry
-
-    lax.fori_loop(0, chunks - 1, drain, 0)
-    swap(chunks - 1).wait_send()
+    swapped(0, chunks).wait_send()
+    walled().wait_send()
     for d in range(1, ny):
         send_raw(d).wait_send()
         pass_raw(d).wait_send()
         send_tw(d).wait_send()
         send_part(d).wait_send()
-    for o in range(1, nm):
-        send_wall(o).wait_send()
     halo_each(send_halo1, "wait_send")
     halo_each(send_halo2, "wait_send")
+
+    def finish(c, carry):
+        for d in range(1, ny):
+            for _, take, put, lanes in pieces(c):
+                series[take, lanes] = series[take, lanes] + incoming[d - 1, c, put, :]
+        return carry
+
+    last = summed - 1
+    for d in range(1, ny):
+        send_series(d, 0, last).wait_recv()
+    lax.fori_loop(0, last, finish, 0)
+    for d in range(1, ny):
+        send_series(d, 0, summed).wait_send()
+        send_series(d, last, 1).wait_recv()
+    finish(last, 0)
 
 
 def store(series, state, series_hbm, state_hbm, sem):
@@ -609,7 +647,7 @@
 
 
 def chip_basis(ny, coefs, rows, horizon):
-    kp, rp = pad8(coefs), pad8(rows)
+    kp, rp = pad(coefs, 8), pad(rows, 8)
     freq = np.arange(ny * CORES).reshape(-1, 1, 1, 1, 1, 1)
     d, r, p, s, k = np.indices((2 * ny - 1, rp, CORES, 2, kp), sparse=True)
     chip, core = freq // CORES, freq % CORES
@@ -643,8 +681,9 @@
     halo = HALO_CELLS // LANE
     blocks = points // LANE
     chunks = blocks // BLOCKS_PER_CHUNK
-    kp, rp = pad8(coefs), pad8(rows)
-    k_all, m_all = CORES * 2 * kp, ny * (rp + 8)
+    kp, rp = pad(coefs, 8), pad(rows, 8)
+    k_all, rb = CORES * 2 * kp, pad(rows, 16) + 16
+    summed = chunks - RAW
     seg = 2 * BLOCKS_PER_CHUNK
     width = BLOCKS_PER_CHUNK * LANE
 
@@ -687,49 +726,49 @@
             pltpu.SMEM(neighbors.shape, jnp.int32),
             vmem(2, rows),
             vmem((2 * ny - 1) * rp, k_all),
-            vmem(8 * ny, k_all),
+            vmem(16 * (2 * ny - 1), k_all),
             vmem(chunks, coefs, seg, LANE),
             vmem(chunks, coefs, seg, LANE),
             vmem(k_all, width),
-            pltpu.VMEM((m_all, k_all), BF16),
-            pltpu.VMEM((m_all, k_all), BF16),
-            pltpu.VMEM((far, rp, k_all), BF16),
-            pltpu.VMEM((far, rp, k_all), BF16),
-            vmem(far, coefs, seg, LANE),
-            vmem(far, coefs, seg, LANE),
+            pltpu.VMEM((ny * rb, k_all), BF16),
+            pltpu.VMEM((ny * rb, k_all), BF16),
+            pltpu.VMEM((far, rb, k_all), BF16),
+            pltpu.VMEM((far, rb, k_all), BF16),
+            vmem(far, RAW, coefs, seg, LANE),
+            vmem(far, RAW, coefs, seg, LANE),
             vmem(far, 2, rows),
-            vmem(far, chunks, rows, width),
-            vmem(far, chunks, rows, width),
-            vmem(ny, 2 * blocks, LANE),
-            vmem(far, 2 * blocks, LANE),
-            vmem(nm * 2 * blocks, LANE),
-            vmem(2 * groups, LANE),
-            pltpu.VMEM((2 * LANE, 2 * groups), BF16),
-            pltpu.VMEM((LANE, 2 * groups), BF16),
+            vmem(far, summed, BLOCKS_PER_CHUNK * rows, LANE),
+            vmem(far, summed, BLOCKS_PER_CHUNK * rows, LANE),
+            vmem(ny, 2, blocks, LANE),
+            vmem(far, 2, summed * BLOCKS_PER_CHUNK, LANE),
+            vmem(2, nm * blocks, LANE),
+            vmem(2, groups, LANE),
             vmem(2, LANE, groups),
-            vmem(groups, LANE, LANE),
+            vmem(2, LANE, groups),
+            vmem(groups, LANE + 8, LANE),
+            vmem(LANE * LANE, groups),
             vmem(2 * cell_rows, LANE),
             vmem(4 * cell_rows, LANE),
             vmem(2, 2 * halo, LANE),
             vmem(2, halo, LANE),
             vmem(cell_rows + 2 * halo, LANE),
             vmem(4, cell_rows, LANE),
-            dma(chunks),
-            dma(chunks),
-            dma(chunks),
-            dma(8),
+            dma(2),
+            dma(1),
+            dma(chunks // PAIR),
+            dma(7),
             dma(far),
             dma(far),
             dma(far),
             dma(far),
             dma(far),
             dma(far),
-            dma(far, chunks),
-            dma(far, chunks),
+            dma(far),
+            dma(far, 2),
             dma(far),
             dma(far),
-            dma(max(nm - 1, 1)),
-            dma(max(nm - 1, 1)),
+            dma(1),
+            dma(1),
             dma(4),
             dma(4),
             pltpu.SemaphoreType.REGULAR,
@@ -738,7 +777,7 @@
             pltpu.SemaphoreType.REGULAR,
         ],
         compiler_params=pltpu.CompilerParams(
-            collective_id=0, has_side_effects=True, vmem_limit_bytes=40000 * 1024
+            collective_id=0, has_side_effects=True, vmem_limit_bytes=50000 * 1024
         ),
         name="adjoint",
     )(group_count, *pinned)

time: 48.4 us -> 46.6 us (0.963)
  Pallas kernels: 46.8 us -> 45 us
    pallas_call x1, Pallas kernels: 45.4 us -> 43.6 us  [local(): pl.pallas_call(functools.partial(kernel, (ny, nm, coefs, rows, chunks)),...]
where the time goes in v3:
time: 46.6 us; the launch traced here: 46.3 us
  Pallas kernels  45 us (97%)
  between operations  1.29 us (3%)
    pallas_call x1, Pallas kernels, local(): pl.pallas_call(functools.partial(kernel, (ny, nm, coefs, rows, chunks)),...  43.6 us
    pallas_call x1, Pallas kernels, local(): pl.pallas_call(store, out_shape=outs, in_specs=[pl.BlockSpec(memory_space...  1.42 us

profile of v3, /device:TPU:0, one launch (start us, length us, event | category | flops | bytes accessed | tf_op | source)
XLA Modules:
  0.0 46.3 jit_solution(5190142170378912547)
XLA Ops:
  1.3 43.6 %adjoint.1 = (f32[108,4096]{1,0:T(8,128)S(1)}, f32[1024,128]{1,0:T(8,128)S(1)}) custom-call(s32[1]{0:T(128)S(6)} %copy.15.count_smem, s32[128]{0:T(128)} %block_hbm.1, s32[4,512]{1,0:T(4,128)} %neigh_hbm.1, f32[2,108]{1,0:T(2,128)} %tw_hbm.1, f32[4,336,224]{2,1,0:T(8,128)} %constant.2.clone.basis_hbm, f32[54,64,128]{2,1,0:T(8,128)} %bitcast.20, ...), custom_call_target="tpu_custom_call" | custom-call | tf_op jit(solution)/shard_map/adjoint/pallas_call | solution.py:719
  44.9 1.4 %store.1 = (f32[108,4096]{1,0:T(8,128)}, f32[1024,128]{1,0:T(8,128)}) custom-call(f32[108,4096]{1,0:T(8,128)S(1)} %get-tuple-element.6.series, f32[1024,128]{1,0:T(8,128)S(1)} %get-tuple-element.7.state), custom_call_target="tpu_custom_call" | custom-call | tf_op jit(solution)/shard_map/store/pallas_call | solution.py:784

commit v4 on v3

v4 whole, which is shorter than its diff:
```python
import functools
import math

import jax
import jax.numpy as jnp
import numpy as np
from jax import lax
from jax.experimental import pallas as pl
from jax.experimental.pallas import tpu as pltpu
from jax.sharding import PartitionSpec as P

LANE = 128
CORES = 2
HALO_CELLS = 4096
BLOCKS_PER_CHUNK = 4
RAW = 2
PAIR = 2
HIGHEST = lax.Precision.HIGHEST
F32 = jnp.float32
BF16 = jnp.bfloat16


def pad(n, to):
    return (n + to - 1) // to * to


def split(x):
    high = x.astype(BF16)
    return high, (x - high.astype(F32)).astype(BF16)


def dot(a, b):
    return jnp.dot(a, b, preferred_element_type=F32)


def kernel(
    dims,
    count_smem,
    block_hbm,
    neigh_hbm,
    tw_hbm,
    basis_hbm,
    spec_hbm,
    weights_hbm,
    wave_hbm,
    coup_hbm,
    series,
    state,
    block_smem,
    neigh_smem,
    tw_own,
    basis_own,
    folded,
    own_spec,
    peer_spec,
    staged,
    lhs_high,
    lhs_low,
    cross_high,
    cross_low,
    raw,
    raw_peer,
    tw_all,
    outgoing,
    incoming,
    part,
    part_in,
    wall,
    picked,
    asked,
    turned,
    weights,
    lined,
    wave,
    coup,
    halo1,
    halo2,
    ext,
    gathered,
    ser_send,
    ser_recv,
):
    ny, nm, coefs, rows, chunks = dims
    groups = weights.shape[0]
    kp, rp, fb = pad(coefs, 8), pad(rows, 8), pad(rows, 16)
    rb = fb + 16
    m1 = ny * rp
    per = part.shape[2]
    cell_rows = ext.shape[0] - 2 * halo1.shape[1] // 2
    halo = halo1.shape[1] // 2
    width = BLOCKS_PER_CHUNK * LANE
    seg = 2 * BLOCKS_PER_CHUNK
    summed = chunks - RAW
    whole_rows = rows // 8 * 8
    rest = rows - whole_rows

    freq = lax.axis_index("freq")
    me = lax.axis_index("mesh")
    chip, core = freq // CORES, freq % CORES
    partner = chip * CORES + (1 - core)

    def at_chip(d):
        return ((chip + d + ny) % ny) * CORES + core

    def peer(d):
        return (me + d + nm) % nm

    def remote(src, dst, send, recv, axis, target):
        return pltpu.make_async_remote_copy(
            src_ref=src,
            dst_ref=dst,
            send_sem=send,
            recv_sem=recv,
            device_id={axis: target},
            device_id_type=pl.DeviceIdType.MESH,
        )

    def send_series(d, first, count):
        span = pl.ds(first, count)
        return remote(
            outgoing.at[d - 1, span],
            incoming.at[d - 1, span],
            ser_send.at[d - 1],
            ser_recv.at[d - 1, jnp.where(first == summed - 1, 1, 0)],
            "freq",
            at_chip(d),
        )

    def pieces(c):
        for j in range(BLOCKS_PER_CHUNK):
            lanes = pl.ds(pl.multiple_of(c * width + j * LANE, LANE), LANE)
            yield j, slice(0, whole_rows), slice(j * whole_rows, (j + 1) * whole_rows), lanes
            if rest:
                first = BLOCKS_PER_CHUNK * whole_rows + j * rest
                yield j, slice(whole_rows, rows), slice(first, first + rest), lanes

    def exchange(
        spec_sem,
        swap_send,
        swap_recv,
        load_sem,
        tw_send,
        tw_recv,
        raw_send,
        raw_recv,
        pass_send,
        pass_recv,
        part_send,
        part_recv,
        wall_send,
        wall_recv,
        halo_send,
        halo_recv,
        go,
        seen,
        peers_in,
        all_in,
    ):
        def load_spec(c):
            return pltpu.make_async_copy(
                spec_hbm.at[:, pl.ds(c * seg, seg), :],
                own_spec.at[c],
                spec_sem.at[1 if c >= summed else 0],
            )

        def loaded(first, count, sem):
            span = own_spec.at[pl.ds(first, count)]
            return pltpu.make_async_copy(span, span, spec_sem.at[sem])

        def swap(c):
            return remote(
                spec_hbm.at[:, pl.ds(c * seg, seg), :],
                peer_spec.at[c],
                swap_send.at[0],
                swap_recv.at[c // PAIR],
                "freq",
                partner,
            )

        def swapped(first, count):
            span = peer_spec.at[pl.ds(first, count)]
            return remote(span, span, swap_send.at[0], swap_recv.at[first // PAIR], "freq", partner)

        def send_tw(d):
            return remote(
                tw_own, tw_all.at[d - 1], tw_send.at[d - 1], tw_recv.at[d - 1], "freq", at_chip(-d)
            )

        def send_raw(d):
            return remote(
                own_spec.at[pl.ds(summed, RAW)],
                raw.at[d - 1],
                raw_send.at[d - 1],
                raw_recv.at[d - 1],
                "freq",
                at_chip(d),
            )

        def pass_raw(d):
            return remote(
                raw.at[d - 1],
                raw_peer.at[d - 1],
                pass_send.at[d - 1],
                pass_recv.at[d - 1],
                "freq",
                partner,
            )

        def send_part(d):
            return remote(
                part.at[d, :, pl.ds(0, summed * BLOCKS_PER_CHUNK), :],
                part_in.at[d - 1],
                part_send.at[d - 1],
                part_recv.at[d - 1],
                "freq",
                at_chip(d),
            )

        def send_wall(o):
            mine = wall.at[:, pl.ds(pl.multiple_of(me * per, 8), per), :]
            return remote(mine, mine, wall_send.at[0], wall_recv.at[0], "mesh", peer(o))

        def walled():
            span = wall.at[:, pl.ds(0, (nm - 1) * per), :]
            return remote(span, span, wall_send.at[0], wall_recv.at[0], "mesh", peer(1))

        def send_halo1(side):
            first = 0 if side else 2 * (cell_rows - halo)
            return remote(
                wave.at[pl.ds(first, 2 * halo)],
                halo1.at[side],
                halo_send.at[side],
                halo_recv.at[side],
                "mesh",
                peer(-1 if side else 1),
            )

        def send_halo2(side):
            first = halo if side else cell_rows
            return remote(
                ext.at[pl.ds(first, halo)],
                halo2.at[side],
                halo_send.at[2 + side],
                halo_recv.at[2 + side],
                "mesh",
                peer(-1 if side else 1),
            )

        inside = (me > 0, me < nm - 1)

        def halo_each(copy, method):
            for side in range(2):
                there = inside[side] if method == "wait_recv" else inside[1 - side]
                pl.when(there)(getattr(copy(side), method))

        def columns(c):
            return pl.ds(pl.multiple_of(c * width, width), width)

        load_wave = pltpu.make_async_copy(wave_hbm, wave, load_sem.at[0])
        load_coup = pltpu.make_async_copy(coup_hbm, coup, load_sem.at[1])
        load_weights = pltpu.make_async_copy(
            weights_hbm, weights.at[:, pl.ds(0, LANE), :], load_sem.at[2]
        )
        load_tw = pltpu.make_async_copy(tw_hbm, tw_own, load_sem.at[3])
        load_basis = pltpu.make_async_copy(basis_hbm.at[freq], basis_own, load_sem.at[4])
        load_neigh = pltpu.make_async_copy(neigh_hbm, neigh_smem, load_sem.at[5])
        load_block = pltpu.make_async_copy(block_hbm, block_smem, load_sem.at[6])

        load_tw.start()
        for c in (*range(summed, chunks), *range(summed)):
            load_spec(c).start()
        load_basis.start()
        load_wave.start()
        load_neigh.start()
        load_block.start()

        barrier = pltpu.get_barrier_semaphore()
        first_core, first_chip = core == 0, chip == 0
        other_core, other_chip = core == 1, chip != 0

        def signal(sem, axis, target):
            pl.semaphore_signal(
                sem, inc=1, device_id={axis: target}, device_id_type=pl.DeviceIdType.MESH
            )

        @pl.when(first_core)
        def _():
            for d in range(1, ny):
                signal(barrier, "freq", at_chip(d))

        @pl.when(first_core == other_chip)
        def _():
            signal(barrier, "freq", partner)

        @pl.when(first_core & first_chip)
        def _():
            pl.semaphore_wait(barrier, ny)
            signal(go.at[0], "freq", partner)

        @pl.when(first_core & other_chip)
        def _():
            pl.semaphore_wait(barrier, ny - 1)

        @pl.when(other_core & other_chip)
        def _():
            pl.semaphore_wait(barrier, 1)
            signal(go.at[0], "freq", partner)

        load_tw.wait()
        loaded(summed, RAW, 1).wait()

        def send_first():
            for d in range(1, ny):
                send_tw(d).start()
                send_raw(d).start()

        pl.when(first_core)(send_first)

        @pl.when(first_core == other_chip)
        def _():
            pl.semaphore_wait(go.at[0], 1)

        for c in range(chunks):
            swap(c).start()

        @pl.when(first_core)
        def _():
            for d in range(1, ny):
                signal(seen.at[d - 1], "freq", at_chip(d))
            for d in range(1, ny):
                pl.semaphore_wait(seen.at[d - 1], 1)
            signal(peers_in.at[0], "freq", partner)

        @pl.when(other_core)
        def _():
            pl.semaphore_wait(peers_in.at[0], 1)
            send_first()

        @pl.when(other_core & first_chip)
        def _():
            for o in range(1, nm):
                signal(barrier, "mesh", peer(o))

        load_coup.start()
        load_weights.start()

        staged[...] = jnp.zeros_like(staged)
        folded[...] = jnp.zeros_like(folded)
        load_basis.wait()
        for d in range(ny):
            high, low = split(basis_own[d * rp : (d + 1) * rp, :])
            lhs_high[d * rb : d * rb + rp, :] = high
            lhs_low[d * rb : d * rb + rp, :] = low
        for d in range(1, ny):
            high, low = split(basis_own[m1 + (d - 1) * rp : m1 + d * rp, :])
            cross_high[d - 1, 0:rp, :] = high
            cross_low[d - 1, 0:rp, :] = low
        for d in range(2 * ny - 1):
            if 0 < d < ny:
                send_tw(d).wait_recv()
            folded[16 * d : 16 * d + 2, :] = jnp.dot(
                tw_all[d - 1] if 0 < d < ny else tw_own[...],
                basis_own[d * rp : d * rp + rows, :],
                precision=HIGHEST,
                preferred_element_type=F32,
            )
            high, low = split(folded[16 * d : 16 * (d + 1), :])
            if d < ny:
                lhs_high[d * rb + fb : (d + 1) * rb, :] = high
                lhs_low[d * rb + fb : (d + 1) * rb, :] = low
            else:
                cross_high[d - ny, fb:rb, :] = high
                cross_low[d - ny, fb:rb, :] = low

        own_rows = own_spec.reshape(chunks * coefs * seg, LANE)
        peer_rows = peer_spec.reshape(chunks * coefs * seg, LANE)
        far = max(ny - 1, 1)
        raw_rows = raw.reshape(far * RAW * coefs * seg, LANE)
        raw_peer_rows = raw_peer.reshape(far * RAW * coefs * seg, LANE)

        def stage(sources, c):
            for p, source in enumerate(sources):
                for s in range(2):
                    for j in range(BLOCKS_PER_CHUNK):
                        piece = source[pl.ds(c * (coefs * seg) + 2 * j + s, coefs, stride=seg), :]
                        base = (p * 2 + s) * kp
                        staged[base : base + coefs, j * LANE : (j + 1) * LANE] = piece
            return split(staged[...])

        def product(high, low, s_high, s_low):
            return dot(high, s_high) + dot(low, s_high) + dot(high, s_low)

        def keep_part(c, total, d):
            for s in range(2):
                row = d * rb + fb + s
                for j in range(BLOCKS_PER_CHUNK):
                    part[d, s, pl.ds(c * BLOCKS_PER_CHUNK + j, 1), :] = total[
                        row : row + 1, j * LANE : (j + 1) * LANE
                    ]

        def summed_chunk(c, carry):
            @pl.when(c % PAIR == 0)
            def _():
                swapped(c, PAIR).wait_recv()

            s_high, s_low = stage((own_rows, peer_rows), c)
            total = product(lhs_high[...], lhs_low[...], s_high, s_low)
            series[:, columns(c)] = total[0:rows]
            keep_part(c, total, 0)
            for d in range(1, ny):
                keep_part(c, total, d)
                for j, take, put, _ in pieces(c):
                    outgoing[d - 1, c, put, :] = total[
                        d * rb + take.start : d * rb + take.stop, j * LANE : (j + 1) * LANE
                    ]
            return carry

        loaded(0, summed, 0).wait()
        lax.fori_loop(0, summed, summed_chunk, 0)
        for d in range(1, ny):
            send_part(d).start()

        def send_chunk(c, carry):
            for d in range(1, ny):
                send_series(d, c, 1).start()
            return carry

        lax.fori_loop(0, summed, send_chunk, 0)

        def raw_chunk(c, carry):
            @pl.when(c % PAIR == 0)
            def _():
                swapped(c, PAIR).wait_recv()

            s_high, s_low = stage((own_rows, peer_rows), c)
            total = product(lhs_high[0:rb, :], lhs_low[0:rb, :], s_high, s_low)
            series[:, columns(c)] = total[0:rows]
            keep_part(c, total, 0)
            return carry

        lax.fori_loop(summed, chunks, raw_chunk, 0)

        @pl.when(other_core & first_chip)
        def _():
            pl.semaphore_wait(barrier, nm - 1)
            for d in range(ny):
                signal(all_in.at[0], "freq", d * CORES)
                if d:
                    signal(all_in.at[0], "freq", d * CORES + 1)

        @pl.when(first_core | other_chip)
        def _():
            pl.semaphore_wait(all_in.at[0], 1)

        load_wave.wait()
        halo_each(send_halo1, "start")

        pitch = weights.shape[1]
        weight_rows = weights.reshape(groups * pitch, LANE)
        load_weights.wait()

        def line_up(t, carry):
            for i in range(4):
                f = t * 4 + i
                lined[pl.ds(pl.multiple_of(f * LANE, LANE), LANE), :] = weight_rows[
                    pl.ds(f, groups, stride=pitch), :
                ].T
            return carry

        lax.fori_loop(0, LANE // 4, line_up, 0)

        for d in range(1, ny):
            send_raw(d).wait_recv()
            pass_raw(d).start()

        wave_rows = 64

        def stage_current(b, carry):
            at = b * wave_rows
            ext[pl.ds(halo + at, wave_rows), :] = wave[pl.ds(2 * at + 1, wave_rows, stride=2), :]
            return carry

        lax.fori_loop(0, cell_rows // wave_rows, stage_current, 0)

        load_neigh.wait()
        load_block.wait()

        def gather():
            def tile(t, carry):
                for n in range(4):
                    for i in range(8):
                        u = t * 8 + i
                        gathered[n, pl.ds(u, 1), :] = ext[pl.ds(neigh_smem[n, u], 1), :]
                return carry

            lax.fori_loop(0, cell_rows // 8, tile, 0)

        def spread_of(at, center):
            total = jnp.zeros((wave_rows, LANE), F32)
            for n in range(4):
                factor = coup[pl.ds(4 * at + n, wave_rows, stride=4), :]
                total += factor * (gathered[n, pl.ds(at, wave_rows), :] - center)
            return total

        inside_low = (jnp.zeros((halo, LANE), jnp.int32) + me) > 0
        inside_high = (jnp.zeros((halo, LANE), jnp.int32) + me) < nm - 1

        halo_each(send_halo1, "wait_recv")
        ext[0:halo, :] = jnp.where(inside_low, halo1[0, pl.ds(1, halo, stride=2), :], 0.0)
        ext[halo + cell_rows :, :] = jnp.where(
            inside_high, halo1[1, pl.ds(1, halo, stride=2), :], 0.0
        )
        load_coup.wait()
        gather()

        def first_step(b, carry):
            at = b * wave_rows
            center = ext[pl.ds(halo + at, wave_rows), :]
            previous = wave[pl.ds(2 * at, wave_rows, stride=2), :]
            state[pl.ds(2 * at, wave_rows, stride=2), :] = (
                2.0 * center - previous + spread_of(at, center)
            )
            return carry

        lax.fori_loop(0, cell_rows // wave_rows, first_step, 0)

        for d in range(1, ny):
            pass_raw(d).wait_recv()
        for r in range(RAW):
            c = summed + r
            total = series[:, columns(c)]
            extra = None
            for d in range(1, ny):
                s_high, s_low = stage((raw_rows, raw_peer_rows), (d - 1) * RAW + r)
                cross = product(cross_high[d - 1], cross_low[d - 1], s_high, s_low)
                total += cross[0:rows]
                extra = cross[fb : fb + 2] if extra is None else extra + cross[fb : fb + 2]
            series[:, columns(c)] = total
            if extra is not None:
                for s in range(2):
                    for j in range(BLOCKS_PER_CHUNK):
                        at = pl.ds(c * BLOCKS_PER_CHUNK + j, 1)
                        part[0, s, at, :] = (
                            part[0, s, at, :] + extra[s : s + 1, j * LANE : (j + 1) * LANE]
                        )

        for d in range(1, ny):
            send_part(d).wait_recv()
        first_blocks = summed * BLOCKS_PER_CHUNK
        base = pl.multiple_of(me * per, 8)
        for s in range(2):
            weighted = part[0, s, 0:first_blocks, :]
            for d in range(1, ny):
                weighted += part_in[d - 1, s]
            wall[s, pl.ds(base, first_blocks), :] = weighted
            wall[s, pl.ds(base + first_blocks, per - first_blocks), :] = part[0, s, first_blocks:, :]
        for o in range(1, nm):
            send_wall(o).start()
        walled().wait_recv()

        def pick(t, carry):
            for i in range(8):
                g = t * 8 + i
                block = block_smem[g]
                for s in range(2):
                    picked[s, pl.ds(g, 1), :] = wall[s, pl.ds(block, 1), :]
            return carry

        lax.fori_loop(0, groups // 8, pick, 0)
        for s in range(2):
            asked[s] = picked[s].T

        def interpolate(t, carry):
            faces = lined[pl.ds(pl.multiple_of(t * 8 * LANE, 8 * LANE), 8 * LANE), :]
            faces = faces.reshape(8, LANE, groups)
            for s in range(2):
                turned[s, pl.ds(pl.multiple_of(t * 8, 8), 8), :] = jnp.sum(
                    faces * asked[s][None], axis=1
                )
            return carry

        lax.fori_loop(0, LANE // 8, interpolate, 0)
        alive = lax.broadcasted_iota(jnp.int32, (groups, LANE), 0) < count_smem[0]
        push = [jnp.where(alive, turned[s].T, 0.0) for s in range(2)]

        top = pl.ds(0, groups, stride=2)
        state[top, :] = state[top, :] + push[0]

        def stage_stepped(b, carry):
            at = b * wave_rows
            ext[pl.ds(halo + at, wave_rows), :] = state[pl.ds(2 * at, wave_rows, stride=2), :]
            return carry

        lax.fori_loop(0, cell_rows // wave_rows, stage_stepped, 0)
        halo_each(send_halo2, "start")
        halo_each(send_halo2, "wait_recv")
        ext[0:halo, :] = jnp.where(inside_low, halo2[0], 0.0)
        ext[halo + cell_rows :, :] = jnp.where(inside_high, halo2[1], 0.0)
        gather()

        def second_step(b, carry):
            at = b * wave_rows
            center = ext[pl.ds(halo + at, wave_rows), :]
            previous = wave[pl.ds(2 * at + 1, wave_rows, stride=2), :]
            state[pl.ds(2 * at + 1, wave_rows, stride=2), :] = (
                2.0 * center - previous + spread_of(at, center)
            )
            return carry

        lax.fori_loop(0, cell_rows // wave_rows, second_step, 0)
        bottom = pl.ds(1, groups, stride=2)
        state[bottom, :] = state[bottom, :] + push[1]

        swapped(0, chunks).wait_send()
        walled().wait_send()
        for d in range(1, ny):
            send_raw(d).wait_send()
            pass_raw(d).wait_send()
            send_tw(d).wait_send()
            send_part(d).wait_send()
        halo_each(send_halo1, "wait_send")
        halo_each(send_halo2, "wait_send")

    dma = lambda *shape: pltpu.SemaphoreType.DMA(shape)
    regular = lambda *shape: pltpu.SemaphoreType.REGULAR(shape)
    far = max(ny - 1, 1)
    pl.run_scoped(
        exchange,
        dma(2),
        dma(1),
        dma(chunks // PAIR),
        dma(7),
        dma(far),
        dma(far),
        dma(far),
        dma(far),
        dma(far),
        dma(far),
        dma(far),
        dma(far),
        dma(1),
        dma(1),
        dma(4),
        dma(4),
        regular(1),
        regular(far),
        regular(1),
        regular(1),
    )

    def finish(c, carry):
        for d in range(1, ny):
            for _, take, put, lanes in pieces(c):
                series[take, lanes] = series[take, lanes] + incoming[d - 1, c, put, :]
        return carry

    last = summed - 1
    for d in range(1, ny):
        send_series(d, 0, last).wait_recv()
    lax.fori_loop(0, last, finish, 0)
    for d in range(1, ny):
        send_series(d, 0, summed).wait_send()
        send_series(d, last, 1).wait_recv()
    finish(last, 0)


def store(series, state, series_hbm, state_hbm, sem):
    copies = [
        pltpu.make_async_copy(series, series_hbm, sem.at[0]),
        pltpu.make_async_copy(state, state_hbm, sem.at[1]),
    ]
    for copy in copies:
        copy.start()
    for copy in copies:
        copy.wait()


def chip_basis(ny, coefs, rows, horizon):
    kp, rp = pad(coefs, 8), pad(rows, 8)
    freq = np.arange(ny * CORES).reshape(-1, 1, 1, 1, 1, 1)
    d, r, p, s, k = np.indices((2 * ny - 1, rp, CORES, 2, kp), sparse=True)
    chip, core = freq // CORES, freq % CORES
    source = chip - np.where(d < ny, 0, d - ny + 1)
    window = ((chip + np.where(d < ny, d, 0)) % ny) * CORES + core
    wave_number = (source % ny * CORES + (core + p) % CORES) * coefs + k
    angle = ((window * rows + r) * wave_number) % horizon * (2.0 * math.pi / horizon)
    scale = np.where(wave_number == 0, 1.0, 2.0) / horizon
    value = np.where(s == 0, np.cos(angle), -np.sin(angle)) * scale
    value = np.where((r < rows) & (k < coefs), value, 0.0)
    return value.reshape(ny * CORES, (2 * ny - 1) * rp, CORES * 2 * kp).astype(np.float32)


def local(
    ny,
    nm,
    spectrum,
    time_weights,
    interp_weights,
    group_block,
    group_count,
    wave_state,
    neighbors,
    coupling,
):
    coefs, points = spectrum.shape[1:]
    rows = time_weights.shape[1]
    horizon = rows * ny * CORES
    groups = interp_weights.shape[0]
    cell_rows = neighbors.shape[1]
    halo = HALO_CELLS // LANE
    blocks = points // LANE
    chunks = blocks // BLOCKS_PER_CHUNK
    kp, rp = pad(coefs, 8), pad(rows, 8)
    k_all, rb = CORES * 2 * kp, pad(rows, 16) + 16
    summed = chunks - RAW
    seg = 2 * BLOCKS_PER_CHUNK
    width = BLOCKS_PER_CHUNK * LANE

    spec = spectrum.reshape(2, coefs, blocks, LANE).transpose(1, 2, 0, 3)
    spec = spec.reshape(coefs, 2 * blocks, LANE)
    wave = wave_state.reshape(2, cell_rows, LANE).transpose(1, 0, 2).reshape(2 * cell_rows, LANE)
    coup = coupling.reshape(4, cell_rows, LANE).transpose(1, 0, 2).reshape(4 * cell_rows, LANE)
    basis = jnp.asarray(chip_basis(ny, coefs, rows, horizon))

    vmem = lambda *shape: pltpu.VMEM(shape, F32)
    dma = lambda *shape: pltpu.SemaphoreType.DMA(shape)
    smem = pl.BlockSpec(memory_space=pltpu.SMEM)
    hbm = pl.BlockSpec(memory_space=pltpu.HBM)
    on_chip = pl.BlockSpec(memory_space=pltpu.VMEM)
    far = max(ny - 1, 1)
    pinned = [
        pltpu.with_memory_space_constraint(x, pltpu.HBM)
        for x in (
            group_block,
            neighbors,
            time_weights,
            basis,
            spec,
            interp_weights,
            wave,
            coup,
        )
    ]
    outs = (
        jax.ShapeDtypeStruct((rows, points), F32),
        jax.ShapeDtypeStruct((2 * cell_rows, LANE), F32),
    )
    series, state = pl.pallas_call(
        functools.partial(kernel, (ny, nm, coefs, rows, chunks)),
        out_shape=outs,
        in_specs=[smem] + [hbm] * 8,
        out_specs=(on_chip, on_chip),
        scratch_shapes=[
            pltpu.SMEM(group_block.shape, jnp.int32),
            pltpu.SMEM(neighbors.shape, jnp.int32),
            vmem(2, rows),
            vmem((2 * ny - 1) * rp, k_all),
            vmem(16 * (2 * ny - 1), k_all),
            vmem(chunks, coefs, seg, LANE),
            vmem(chunks, coefs, seg, LANE),
            vmem(k_all, width),
            pltpu.VMEM((ny * rb, k_all), BF16),
            pltpu.VMEM((ny * rb, k_all), BF16),
            pltpu.VMEM((far, rb, k_all), BF16),
            pltpu.VMEM((far, rb, k_all), BF16),
            vmem(far, RAW, coefs, seg, LANE),
            vmem(far, RAW, coefs, seg, LANE),
            vmem(far, 2, rows),
            vmem(far, summed, BLOCKS_PER_CHUNK * rows, LANE),
            vmem(far, summed, BLOCKS_PER_CHUNK * rows, LANE),
            vmem(ny, 2, blocks, LANE),
            vmem(far, 2, summed * BLOCKS_PER_CHUNK, LANE),
            vmem(2, nm * blocks, LANE),
            vmem(2, groups, LANE),
            vmem(2, LANE, groups),
            vmem(2, LANE, groups),
            vmem(groups, LANE + 8, LANE),
            vmem(LANE * LANE, groups),
            vmem(2 * cell_rows, LANE),
            vmem(4 * cell_rows, LANE),
            vmem(2, 2 * halo, LANE),
            vmem(2, halo, LANE),
            vmem(cell_rows + 2 * halo, LANE),
            vmem(4, cell_rows, LANE),
            dma(far),
            dma(far, 2),
        ],
        compiler_params=pltpu.CompilerParams(
            collective_id=0, has_side_effects=True, vmem_limit_bytes=50000 * 1024
        ),
        name="adjoint",
    )(group_count, *pinned)
    series, state = pl.pallas_call(
        store,
        out_shape=outs,
        in_specs=[pl.BlockSpec(memory_space=pl.ANY)] * 2,
        out_specs=(hbm, hbm),
        scratch_shapes=[dma(2)],
        compiler_params=pltpu.CompilerParams(vmem_limit_bytes=1024 * 1024),
        name="store",
    )(series, state)
    new_state = state.reshape(cell_rows, 2, LANE).transpose(1, 0, 2)
    return series, new_state.reshape(1, 2, cell_rows * LANE)


def solution(mesh):
    placed = (
        P(None, "freq", "mesh"),
        P(None, "freq"),
        P("mesh", None, None),
        P("mesh"),
        P("mesh"),
        P("freq", None, "mesh"),
        P(None, "mesh"),
        P(None, "mesh"),
    )
    ny = mesh.shape["freq"] // CORES
    return jax.shard_map(
        functools.partial(local, ny, mesh.shape["mesh"]),
        mesh=mesh,
        in_specs=placed,
        out_specs=(P("freq", "mesh"), P("freq", None, "mesh")),
        check_vma=False,
    )
```

time: 46.6 us -> 46.3 us (level)
  no operation moved by 1% of the time
where the time goes in v4:
time: 46.3 us; the launch traced here: 46 us
  Pallas kernels  44.7 us (97%)
  between operations  1.29 us (3%)
    pallas_call x1, Pallas kernels, local(): pl.pallas_call(functools.partial(kernel, (ny, nm, coefs, rows, chunks)),...  43.3 us
    pallas_call x1, Pallas kernels, local(): pl.pallas_call(store, out_shape=outs, in_specs=[pl.BlockSpec(memory_space...  1.42 us

profile of v4, /device:TPU:0, one launch (start us, length us, event | category | flops | bytes accessed | tf_op | source)
XLA Modules:
  0.0 46.0 jit_solution(5382709402200045883)
XLA Ops:
  1.3 43.3 %adjoint.1 = (f32[108,4096]{1,0:T(8,128)S(1)}, f32[1024,128]{1,0:T(8,128)S(1)}) custom-call(s32[1]{0:T(128)S(6)} %copy.15.count_smem, s32[128]{0:T(128)} %block_hbm.1, s32[4,512]{1,0:T(4,128)} %neigh_hbm.1, f32[2,108]{1,0:T(2,128)} %tw_hbm.1, f32[4,336,224]{2,1,0:T(8,128)} %constant.2.clone.basis_hbm, f32[54,64,128]{2,1,0:T(8,128)} %bitcast.20, ...), custom_call_target="tpu_custom_call" | custom-call | tf_op jit(solution)/shard_map/adjoint/pallas_call | solution.py:748
  44.6 1.4 %store.1 = (f32[108,4096]{1,0:T(8,128)}, f32[1024,128]{1,0:T(8,128)}) custom-call(f32[108,4096]{1,0:T(8,128)S(1)} %get-tuple-element.6.series, f32[1024,128]{1,0:T(8,128)S(1)} %get-tuple-element.7.state), custom_call_target="tpu_custom_call" | custom-call | tf_op jit(solution)/shard_map/store/pallas_call | solution.py:793

commit v5 on v4

--- a/solution.py
+++ b/solution.py
@@ -183,13 +183,23 @@
 
         def send_tw(d):
             return remote(
-                tw_own, tw_all.at[d - 1], tw_send.at[d - 1], tw_recv.at[d - 1], "freq", at_chip(-d)
+                tw_hbm, tw_all.at[d - 1], tw_send.at[d - 1], tw_recv.at[d - 1], "freq", at_chip(-d)
             )
 
         def send_raw(d):
             return remote(
-                own_spec.at[pl.ds(summed, RAW)],
+                spec_hbm.at[:, pl.ds(summed * seg, RAW * seg), :],
                 raw.at[d - 1],
+                raw_send.at[d - 1],
+                raw_recv.at[d - 1],
+                "freq",
+                at_chip(d),
+            )
+
+        def send_raw_chunk(d, r):
+            return remote(
+                own_spec.at[summed + r],
+                raw.at[d - 1, :, pl.ds(r * seg, seg), :],
                 raw_send.at[d - 1],
                 raw_recv.at[d - 1],
                 "freq",
@@ -266,6 +276,31 @@
         load_neigh = pltpu.make_async_copy(neigh_hbm, neigh_smem, load_sem.at[5])
         load_block = pltpu.make_async_copy(block_hbm, block_smem, load_sem.at[6])
 
+        barrier = pltpu.get_barrier_semaphore()
+        first_core, first_chip = core == 0, chip == 0
+        other_core, other_chip = core == 1, chip != 0
+
+        def signal(sem, axis, target):
+            pl.semaphore_signal(
+                sem, inc=1, device_id={axis: target}, device_id_type=pl.DeviceIdType.MESH
+            )
+
+        @pl.when(first_core)
+        def _():
+            for d in range(1, ny):
+                signal(barrier, "freq", at_chip(d))
+
+        @pl.when(first_core == other_chip)
+        def _():
+            signal(barrier, "freq", partner)
+
+        @pl.when(first_core & other_chip)
+        def _():
+            pl.semaphore_wait(barrier, ny - 1)
+            for d in range(1, ny):
+                send_tw(d).start()
+                send_raw(d).start()
+
         load_tw.start()
         for c in (*range(summed, chunks), *range(summed)):
             load_spec(c).start()
@@ -274,47 +309,24 @@
         load_neigh.start()
         load_block.start()
 
-        barrier = pltpu.get_barrier_semaphore()
-        first_core, first_chip = core == 0, chip == 0
-        other_core, other_chip = core == 1, chip != 0
-
-        def signal(sem, axis, target):
-            pl.semaphore_signal(
-                sem, inc=1, device_id={axis: target}, device_id_type=pl.DeviceIdType.MESH
-            )
-
-        @pl.when(first_core)
-        def _():
-            for d in range(1, ny):
-                signal(barrier, "freq", at_chip(d))
-
-        @pl.when(first_core == other_chip)
-        def _():
-            signal(barrier, "freq", partner)
-
         @pl.when(first_core & first_chip)
         def _():
             pl.semaphore_wait(barrier, ny)
             signal(go.at[0], "freq", partner)
 
-        @pl.when(first_core & other_chip)
-        def _():
-            pl.semaphore_wait(barrier, ny - 1)
-
         @pl.when(other_core & other_chip)
         def _():
             pl.semaphore_wait(barrier, 1)
             signal(go.at[0], "freq", partner)
 
-        load_tw.wait()
-        loaded(summed, RAW, 1).wait()
-
-        def send_first():
+        def send_loaded():
+            loaded(summed, RAW, 1).wait()
             for d in range(1, ny):
                 send_tw(d).start()
-                send_raw(d).start()
-
-        pl.when(first_core)(send_first)
+                for r in range(RAW):
+                    send_raw_chunk(d, r).start()
+
+        pl.when(first_core & first_chip)(send_loaded)
 
         @pl.when(first_core == other_chip)
         def _():
@@ -334,7 +346,7 @@
         @pl.when(other_core)
         def _():
             pl.semaphore_wait(peers_in.at[0], 1)
-            send_first()
+            send_loaded()
 
         @pl.when(other_core & first_chip)
         def _():
@@ -346,6 +358,7 @@
 
         staged[...] = jnp.zeros_like(staged)
         folded[...] = jnp.zeros_like(folded)
+        load_tw.wait()
         load_basis.wait()
         for d in range(ny):
             high, low = split(basis_own[d * rp : (d + 1) * rp, :])
@@ -378,11 +391,11 @@
         raw_rows = raw.reshape(far * RAW * coefs * seg, LANE)
         raw_peer_rows = raw_peer.reshape(far * RAW * coefs * seg, LANE)
 
-        def stage(sources, c):
+        def stage(sources, first, step=seg):
             for p, source in enumerate(sources):
                 for s in range(2):
                     for j in range(BLOCKS_PER_CHUNK):
-                        piece = source[pl.ds(c * (coefs * seg) + 2 * j + s, coefs, stride=seg), :]
+                        piece = source[pl.ds(first + 2 * j + s, coefs, stride=step), :]
                         base = (p * 2 + s) * kp
                         staged[base : base + coefs, j * LANE : (j + 1) * LANE] = piece
             return split(staged[...])
@@ -403,7 +416,7 @@
             def _():
                 swapped(c, PAIR).wait_recv()
 
-            s_high, s_low = stage((own_rows, peer_rows), c)
+            s_high, s_low = stage((own_rows, peer_rows), c * (coefs * seg))
             total = product(lhs_high[...], lhs_low[...], s_high, s_low)
             series[:, columns(c)] = total[0:rows]
             keep_part(c, total, 0)
@@ -416,6 +429,11 @@
             return carry
 
         loaded(0, summed, 0).wait()
+
+        @pl.when(first_core & other_chip)
+        def _():
+            loaded(summed, RAW, 1).wait()
+
         lax.fori_loop(0, summed, summed_chunk, 0)
         for d in range(1, ny):
             send_part(d).start()
@@ -432,7 +450,7 @@
             def _():
                 swapped(c, PAIR).wait_recv()
 
-            s_high, s_low = stage((own_rows, peer_rows), c)
+            s_high, s_low = stage((own_rows, peer_rows), c * (coefs * seg))
             total = product(lhs_high[0:rb, :], lhs_low[0:rb, :], s_high, s_low)
             series[:, columns(c)] = total[0:rows]
             keep_part(c, total, 0)
@@ -531,7 +549,9 @@
             total = series[:, columns(c)]
             extra = None
             for d in range(1, ny):
-                s_high, s_low = stage((raw_rows, raw_peer_rows), (d - 1) * RAW + r)
+                s_high, s_low = stage(
+                    (raw_rows, raw_peer_rows), ((d - 1) * coefs * RAW + r) * seg, RAW * seg
+                )
                 cross = product(cross_high[d - 1], cross_low[d - 1], s_high, s_low)
                 total += cross[0:rows]
                 extra = cross[fb : fb + 2] if extra is None else extra + cross[fb : fb + 2]
@@ -763,8 +783,8 @@
             pltpu.VMEM((ny * rb, k_all), BF16),
             pltpu.VMEM((far, rb, k_all), BF16),
             pltpu.VMEM((far, rb, k_all), BF16),
-            vmem(far, RAW, coefs, seg, LANE),
-            vmem(far, RAW, coefs, seg, LANE),
+            vmem(far, coefs, RAW * seg, LANE),
+            vmem(far, coefs, RAW * seg, LANE),
             vmem(far, 2, rows),
             vmem(far, summed, BLOCKS_PER_CHUNK * rows, LANE),
             vmem(far, summed, BLOCKS_PER_CHUNK * rows, LANE),

time: 46.3 us -> 45.5 us (0.983)
  Pallas kernels: 44.7 us -> 43.9 us
    pallas_call x1, Pallas kernels: 43.3 us -> 42.5 us  [local(): pl.pallas_call(functools.partial(kernel, (ny, nm, coefs, rows, chunks)),...]
where the time goes in v5:
time: 45.5 us; the launch traced here: 45.2 us
  Pallas kernels  43.9 us (96%)
  between operations  1.29 us (3%)
    pallas_call x1, Pallas kernels, local(): pl.pallas_call(functools.partial(kernel, (ny, nm, coefs, rows, chunks)),...  42.5 us
    pallas_call x1, Pallas kernels, local(): pl.pallas_call(store, out_shape=outs, in_specs=[pl.BlockSpec(memory_space...  1.42 us

profile of v5, /device:TPU:0, one launch (start us, length us, event | category | flops | bytes accessed | tf_op | source)
XLA Modules:
  0.0 45.2 jit_solution(3584068254240941070)
XLA Ops:
  1.3 42.5 %adjoint.1 = (f32[108,4096]{1,0:T(8,128)S(1)}, f32[1024,128]{1,0:T(8,128)S(1)}) custom-call(s32[1]{0:T(128)S(6)} %copy.15.count_smem, s32[128]{0:T(128)} %block_hbm.1, s32[4,512]{1,0:T(4,128)} %neigh_hbm.1, f32[2,108]{1,0:T(2,128)} %tw_hbm.1, f32[4,336,224]{2,1,0:T(8,128)} %constant.2.clone.basis_hbm, f32[54,64,128]{2,1,0:T(8,128)} %bitcast.20, ...), custom_call_target="tpu_custom_call" | custom-call | tf_op jit(solution)/shard_map/adjoint/pallas_call | solution.py:768
  43.8 1.4 %store.1 = (f32[108,4096]{1,0:T(8,128)}, f32[1024,128]{1,0:T(8,128)}) custom-call(f32[108,4096]{1,0:T(8,128)S(1)} %get-tuple-element.6.series, f32[1024,128]{1,0:T(8,128)S(1)} %get-tuple-element.7.state), custom_call_target="tpu_custom_call" | custom-call | tf_op jit(solution)/shard_map/store/pallas_call | solution.py:813

commit v6 on v5

--- a/solution.py
+++ b/solution.py
@@ -153,7 +153,6 @@
         halo_recv,
         go,
         seen,
-        peers_in,
         all_in,
     ):
         def load_spec(c):
@@ -169,7 +168,7 @@
 
         def swap(c):
             return remote(
-                spec_hbm.at[:, pl.ds(c * seg, seg), :],
+                own_spec.at[c],
                 peer_spec.at[c],
                 swap_send.at[0],
                 swap_recv.at[c // PAIR],
@@ -285,21 +284,27 @@
                 sem, inc=1, device_id={axis: target}, device_id_type=pl.DeviceIdType.MESH
             )
 
-        @pl.when(first_core)
-        def _():
-            for d in range(1, ny):
+        for d in range(1, ny):
+            at_first = at_chip(d) < CORES
+
+            @pl.when(first_core | jnp.logical_not(at_first))
+            def _():
                 signal(barrier, "freq", at_chip(d))
 
-        @pl.when(first_core == other_chip)
+        @pl.when(other_core)
         def _():
             signal(barrier, "freq", partner)
 
-        @pl.when(first_core & other_chip)
-        def _():
-            pl.semaphore_wait(barrier, ny - 1)
+        @pl.when(other_chip)
+        def _():
+            pl.semaphore_wait(barrier, jnp.where(first_core, ny, ny - 1))
             for d in range(1, ny):
                 send_tw(d).start()
                 send_raw(d).start()
+
+        @pl.when(other_core & other_chip)
+        def _():
+            signal(seen.at[chip - 1], "freq", 1)
 
         load_tw.start()
         for c in (*range(summed, chunks), *range(summed)):
@@ -309,44 +314,39 @@
         load_neigh.start()
         load_block.start()
 
-        @pl.when(first_core & first_chip)
-        def _():
-            pl.semaphore_wait(barrier, ny)
-            signal(go.at[0], "freq", partner)
-
-        @pl.when(other_core & other_chip)
-        def _():
-            pl.semaphore_wait(barrier, 1)
-            signal(go.at[0], "freq", partner)
-
-        def send_loaded():
+        @pl.when(first_chip)
+        def _():
+            @pl.when(first_core)
+            def _():
+                pl.semaphore_wait(barrier, ny)
+
+            @pl.when(other_core)
+            def _():
+                for d in range(1, ny):
+                    pl.semaphore_wait(seen.at[d - 1], 1)
+
             loaded(summed, RAW, 1).wait()
             for d in range(1, ny):
                 send_tw(d).start()
                 for r in range(RAW):
                     send_raw_chunk(d, r).start()
 
-        pl.when(first_core & first_chip)(send_loaded)
-
-        @pl.when(first_core == other_chip)
+        @pl.when(first_core)
+        def _():
+            signal(go.at[0], "freq", partner)
+
+        @pl.when(other_core)
         def _():
             pl.semaphore_wait(go.at[0], 1)
+
+        loaded(0, summed, 0).wait()
+
+        @pl.when(other_chip)
+        def _():
+            loaded(summed, RAW, 1).wait()
 
         for c in range(chunks):
             swap(c).start()
-
-        @pl.when(first_core)
-        def _():
-            for d in range(1, ny):
-                signal(seen.at[d - 1], "freq", at_chip(d))
-            for d in range(1, ny):
-                pl.semaphore_wait(seen.at[d - 1], 1)
-            signal(peers_in.at[0], "freq", partner)
-
-        @pl.when(other_core)
-        def _():
-            pl.semaphore_wait(peers_in.at[0], 1)
-            send_loaded()
 
         @pl.when(other_core & first_chip)
         def _():
@@ -427,12 +427,6 @@
                         d * rb + take.start : d * rb + take.stop, j * LANE : (j + 1) * LANE
                     ]
             return carry
-
-        loaded(0, summed, 0).wait()
-
-        @pl.when(first_core & other_chip)
-        def _():
-            loaded(summed, RAW, 1).wait()
 
         lax.fori_loop(0, summed, summed_chunk, 0)
         for d in range(1, ny):
@@ -664,7 +658,6 @@
         dma(4),
         regular(1),
         regular(far),
-        regular(1),
         regular(1),
     )
 

time: 45.5 us -> 45.3 us (level)
  no operation moved by 1% of the time
where the time goes in v6:
time: 45.3 us; the launch traced here: 45.2 us
  Pallas kernels  43.9 us (97%)
  between operations  1.29 us (3%)
    pallas_call x1, Pallas kernels, local(): pl.pallas_call(functools.partial(kernel, (ny, nm, coefs, rows, chunks)),...  42.5 us
    pallas_call x1, Pallas kernels, local(): pl.pallas_call(store, out_shape=outs, in_specs=[pl.BlockSpec(memory_space...  1.42 us

profile of v6, /device:TPU:0, one launch (start us, length us, event | category | flops | bytes accessed | tf_op | source)
XLA Modules:
  0.0 45.2 jit_solution(2560742836166428387)
XLA Ops:
  1.3 42.5 %adjoint.1 = (f32[108,4096]{1,0:T(8,128)S(1)}, f32[1024,128]{1,0:T(8,128)S(1)}) custom-call(s32[1]{0:T(128)S(6)} %copy.15.count_smem, s32[128]{0:T(128)} %block_hbm.1, s32[4,512]{1,0:T(4,128)} %neigh_hbm.1, f32[2,108]{1,0:T(2,128)} %tw_hbm.1, f32[4,336,224]{2,1,0:T(8,128)} %constant.2.clone.basis_hbm, f32[54,64,128]{2,1,0:T(8,128)} %bitcast.20, ...), custom_call_target="tpu_custom_call" | custom-call | tf_op jit(solution)/shard_map/adjoint/pallas_call | solution.py:761
  43.8 1.4 %store.1 = (f32[108,4096]{1,0:T(8,128)}, f32[1024,128]{1,0:T(8,128)}) custom-call(f32[108,4096]{1,0:T(8,128)S(1)} %get-tuple-element.6.series, f32[1024,128]{1,0:T(8,128)S(1)} %get-tuple-element.7.state), custom_call_target="tpu_custom_call" | custom-call | tf_op jit(solution)/shard_map/store/pallas_call | solution.py:806

commit v7 on v6

--- a/solution.py
+++ b/solution.py
@@ -65,6 +65,7 @@
     incoming,
     part,
     part_in,
+    aside,
     wall,
     picked,
     asked,
@@ -147,6 +148,9 @@
         pass_recv,
         part_send,
         part_recv,
+        aside_send,
+        aside_recv,
+        on_send,
         wall_send,
         wall_recv,
         halo_send,
@@ -225,6 +229,32 @@
                 at_chip(d),
             )
 
+        def detoured(d):
+            return (me == 0) & ((chip + d) % ny == 0)
+
+        def passes():
+            return (me == 1 + core) & (chip == 0)
+
+        def send_aside(d):
+            return pltpu.make_async_remote_copy(
+                src_ref=part.at[d, :, pl.ds(0, summed * BLOCKS_PER_CHUNK), :],
+                dst_ref=aside.at[d - 1],
+                send_sem=aside_send.at[d - 1],
+                recv_sem=aside_recv.at[d - 1],
+                device_id={"freq": at_chip(d), "mesh": 1 + core},
+                device_id_type=pl.DeviceIdType.MESH,
+            )
+
+        def send_on(d):
+            return remote(
+                aside.at[d - 1],
+                part_in.at[d - 1],
+                on_send.at[d - 1],
+                part_recv.at[d - 1],
+                "mesh",
+                0,
+            )
+
         def send_wall(o):
             mine = wall.at[:, pl.ds(pl.multiple_of(me * per, 8), per), :]
             return remote(mine, mine, wall_send.at[0], wall_recv.at[0], "mesh", peer(o))
@@ -430,7 +460,7 @@
 
         lax.fori_loop(0, summed, summed_chunk, 0)
         for d in range(1, ny):
-            send_part(d).start()
+            pl.when(jnp.logical_not(detoured(d)))(send_part(d).start)
 
         def send_chunk(c, carry):
             for d in range(1, ny):
@@ -464,6 +494,8 @@
         def _():
             pl.semaphore_wait(all_in.at[0], 1)
 
+        for d in range(1, ny):
+            pl.when(detoured(d))(send_aside(d).start)
         load_wave.wait()
         halo_each(send_halo1, "start")
 
@@ -559,6 +591,13 @@
                         )
 
         for d in range(1, ny):
+
+            @pl.when(passes())
+            def _():
+                send_aside(d).wait_recv()
+                send_on(d).start()
+
+        for d in range(1, ny):
             send_part(d).wait_recv()
         first_blocks = summed * BLOCKS_PER_CHUNK
         base = pl.multiple_of(me * per, 8)
@@ -631,7 +670,9 @@
             send_raw(d).wait_send()
             pass_raw(d).wait_send()
             send_tw(d).wait_send()
-            send_part(d).wait_send()
+            pl.when(jnp.logical_not(detoured(d)))(send_part(d).wait_send)
+            pl.when(detoured(d))(send_aside(d).wait_send)
+            pl.when(passes())(send_on(d).wait_send)
         halo_each(send_halo1, "wait_send")
         halo_each(send_halo2, "wait_send")
 
@@ -644,6 +685,9 @@
         dma(1),
         dma(chunks // PAIR),
         dma(7),
+        dma(far),
+        dma(far),
+        dma(far),
         dma(far),
         dma(far),
         dma(far),
@@ -783,6 +827,7 @@
             vmem(far, summed, BLOCKS_PER_CHUNK * rows, LANE),
             vmem(ny, 2, blocks, LANE),
             vmem(far, 2, summed * BLOCKS_PER_CHUNK, LANE),
+            vmem(far, 2, summed * BLOCKS_PER_CHUNK, LANE),
             vmem(2, nm * blocks, LANE),
             vmem(2, groups, LANE),
             vmem(2, LANE, groups),

time: 45.3 us -> 44.8 us (0.989)
  Pallas kernels: 43.9 us -> 43.4 us
    pallas_call x1, Pallas kernels: 42.5 us -> 42 us  [local(): pl.pallas_call(functools.partial(kernel, (ny, nm, coefs, rows, chunks)),...]
where the time goes in v7:
time: 44.8 us; the launch traced here: 44.7 us
  Pallas kernels  43.4 us (97%)
  between operations  1.29 us (3%)
    pallas_call x1, Pallas kernels, local(): pl.pallas_call(functools.partial(kernel, (ny, nm, coefs, rows, chunks)),...  42 us
    pallas_call x1, Pallas kernels, local(): pl.pallas_call(store, out_shape=outs, in_specs=[pl.BlockSpec(memory_space...  1.42 us

profile of v7, /device:TPU:0, one launch (start us, length us, event | category | flops | bytes accessed | tf_op | source)
XLA Modules:
  0.0 44.7 jit_solution(16446968854978159965)
XLA Ops:
  1.3 42.0 %adjoint.1 = (f32[108,4096]{1,0:T(8,128)S(1)}, f32[1024,128]{1,0:T(8,128)S(1)}) custom-call(s32[1]{0:T(128)S(6)} %copy.15.count_smem, s32[128]{0:T(128)} %block_hbm.1, s32[4,512]{1,0:T(4,128)} %neigh_hbm.1, f32[2,108]{1,0:T(2,128)} %tw_hbm.1, f32[4,336,224]{2,1,0:T(8,128)} %constant.2.clone.basis_hbm, f32[54,64,128]{2,1,0:T(8,128)} %bitcast.20, ...), custom_call_target="tpu_custom_call" | custom-call | tf_op jit(solution)/shard_map/adjoint/pallas_call | solution.py:805
  43.2 1.4 %store.1 = (f32[108,4096]{1,0:T(8,128)}, f32[1024,128]{1,0:T(8,128)}) custom-call(f32[108,4096]{1,0:T(8,128)S(1)} %get-tuple-element.6.series, f32[1024,128]{1,0:T(8,128)S(1)} %get-tuple-element.7.state), custom_call_target="tpu_custom_call" | custom-call | tf_op jit(solution)/shard_map/store/pallas_call | solution.py:851

commit v8 on v6

--- a/solution.py
+++ b/solution.py
@@ -13,8 +13,9 @@
 CORES = 2
 HALO_CELLS = 4096
 BLOCKS_PER_CHUNK = 4
-RAW = 2
+RAW = 3
 PAIR = 2
+HEAD = 32
 HIGHEST = lax.Precision.HIGHEST
 F32 = jnp.float32
 BF16 = jnp.bfloat16
@@ -65,6 +66,8 @@
     incoming,
     part,
     part_in,
+    aside,
+    aside_head,
     wall,
     picked,
     asked,
@@ -115,13 +118,26 @@
             device_id_type=pl.DeviceIdType.MESH,
         )
 
+    last = summed - 1
+
     def send_series(d, first, count):
         span = pl.ds(first, count)
         return remote(
             outgoing.at[d - 1, span],
             incoming.at[d - 1, span],
-            ser_send.at[d - 1],
-            ser_recv.at[d - 1, jnp.where(first == summed - 1, 1, 0)],
+            ser_send.at[d - 1, 0],
+            ser_recv.at[d - 1, 0],
+            "freq",
+            at_chip(d),
+        )
+
+    def send_last(d):
+        span = pl.ds(HEAD, outgoing.shape[2] - HEAD)
+        return remote(
+            outgoing.at[d - 1, last, span],
+            incoming.at[d - 1, last, span],
+            ser_send.at[d - 1, 1],
+            ser_recv.at[d - 1, 1],
             "freq",
             at_chip(d),
         )
@@ -147,6 +163,11 @@
         pass_recv,
         part_send,
         part_recv,
+        aside_send,
+        aside_recv,
+        on_send,
+        head_send,
+        head_recv,
         wall_send,
         wall_recv,
         halo_send,
@@ -225,6 +246,52 @@
                 at_chip(d),
             )
 
+        def detoured(d):
+            return (me == 0) & ((chip + d) % ny == 0)
+
+        def passes():
+            return (me == 1 + core) & (chip == 0)
+
+        def head(ref, d):
+            return ref.at[d - 1, last, pl.ds(0, HEAD)]
+
+        def send_head(d):
+            return remote(
+                head(outgoing, d),
+                head(incoming, d),
+                head_send.at[d - 1],
+                head_recv.at[d - 1],
+                "freq",
+                at_chip(d),
+            )
+
+        def send_aside(d):
+            pairs = (
+                (part.at[d, :, pl.ds(0, summed * BLOCKS_PER_CHUNK), :], aside),
+                (head(outgoing, d), aside_head),
+            )
+            return [
+                pltpu.make_async_remote_copy(
+                    src_ref=source,
+                    dst_ref=target.at[d - 1],
+                    send_sem=aside_send.at[d - 1, i],
+                    recv_sem=aside_recv.at[d - 1, i],
+                    device_id={"freq": at_chip(d), "mesh": 1 + core},
+                    device_id_type=pl.DeviceIdType.MESH,
+                )
+                for i, (source, target) in enumerate(pairs)
+            ]
+
+        def send_on(d):
+            pairs = (
+                (aside.at[d - 1], part_in.at[d - 1], part_recv),
+                (aside_head.at[d - 1], head(incoming, d), head_recv),
+            )
+            return [
+                remote(source, target, on_send.at[d - 1, i], recv.at[d - 1], "mesh", 0)
+                for i, (source, target, recv) in enumerate(pairs)
+            ]
+
         def send_wall(o):
             mine = wall.at[:, pl.ds(pl.multiple_of(me * per, 8), per), :]
             return remote(mine, mine, wall_send.at[0], wall_recv.at[0], "mesh", peer(o))
@@ -430,14 +497,18 @@
 
         lax.fori_loop(0, summed, summed_chunk, 0)
         for d in range(1, ny):
-            send_part(d).start()
+            pl.when(jnp.logical_not(detoured(d)))(send_part(d).start)
 
         def send_chunk(c, carry):
             for d in range(1, ny):
                 send_series(d, c, 1).start()
             return carry
 
-        lax.fori_loop(0, summed, send_chunk, 0)
+        for d in range(1, ny):
+            pl.when(jnp.logical_not(detoured(d)))(send_head(d).start)
+        lax.fori_loop(0, last, send_chunk, 0)
+        for d in range(1, ny):
+            send_last(d).start()
 
         def raw_chunk(c, carry):
             @pl.when(c % PAIR == 0)
@@ -463,6 +534,13 @@
         @pl.when(first_core | other_chip)
         def _():
             pl.semaphore_wait(all_in.at[0], 1)
+
+        for d in range(1, ny):
+
+            @pl.when(detoured(d))
+            def _():
+                for copy in send_aside(d):
+                    copy.start()
 
         load_wave.wait()
         halo_each(send_halo1, "start")
@@ -559,6 +637,15 @@
                         )
 
         for d in range(1, ny):
+
+            @pl.when(passes())
+            def _():
+                for copy in send_aside(d):
+                    copy.wait_recv()
+                for copy in send_on(d):
+                    copy.start()
+
+        for d in range(1, ny):
             send_part(d).wait_recv()
         first_blocks = summed * BLOCKS_PER_CHUNK
         base = pl.multiple_of(me * per, 8)
@@ -631,7 +718,23 @@
             send_raw(d).wait_send()
             pass_raw(d).wait_send()
             send_tw(d).wait_send()
-            send_part(d).wait_send()
+
+            @pl.when(jnp.logical_not(detoured(d)))
+            def _():
+                send_part(d).wait_send()
+                send_head(d).wait_send()
+
+            @pl.when(detoured(d))
+            def _():
+                for copy in send_aside(d):
+                    copy.wait_send()
+
+            @pl.when(passes())
+            def _():
+                for copy in send_on(d):
+                    copy.wait_send()
+
+            send_head(d).wait_recv()
         halo_each(send_halo1, "wait_send")
         halo_each(send_halo2, "wait_send")
 
@@ -652,6 +755,11 @@
         dma(far),
         dma(far),
         dma(far),
+        dma(far, 2),
+        dma(far, 2),
+        dma(far, 2),
+        dma(far),
+        dma(far),
         dma(1),
         dma(1),
         dma(4),
@@ -667,13 +775,13 @@
                 series[take, lanes] = series[take, lanes] + incoming[d - 1, c, put, :]
         return carry
 
-    last = summed - 1
     for d in range(1, ny):
         send_series(d, 0, last).wait_recv()
     lax.fori_loop(0, last, finish, 0)
     for d in range(1, ny):
-        send_series(d, 0, summed).wait_send()
-        send_series(d, last, 1).wait_recv()
+        send_series(d, 0, last).wait_send()
+        send_last(d).wait_send()
+        send_last(d).wait_recv()
     finish(last, 0)
 
 
@@ -783,6 +891,8 @@
             vmem(far, summed, BLOCKS_PER_CHUNK * rows, LANE),
             vmem(ny, 2, blocks, LANE),
             vmem(far, 2, summed * BLOCKS_PER_CHUNK, LANE),
+            vmem(far, 2, summed * BLOCKS_PER_CHUNK, LANE),
+            vmem(far, HEAD, LANE),
             vmem(2, nm * blocks, LANE),
             vmem(2, groups, LANE),
             vmem(2, LANE, groups),
@@ -795,7 +905,7 @@
             vmem(2, halo, LANE),
             vmem(cell_rows + 2 * halo, LANE),
             vmem(4, cell_rows, LANE),
-            dma(far),
+            dma(far, 2),
             dma(far, 2),
         ],
         compiler_params=pltpu.CompilerParams(

time: 45.3 us -> 44.5 us (0.982)
  Pallas kernels: 43.9 us -> 43.1 us
    pallas_call x1, Pallas kernels: 42.5 us -> 41.7 us  [local(): pl.pallas_call(functools.partial(kernel, (ny, nm, coefs, rows, chunks)),...]
where the time goes in v8:
time: 44.5 us; the launch traced here: 44.4 us
  Pallas kernels  43.1 us (97%)
  between operations  1.29 us (3%)
    pallas_call x1, Pallas kernels, local(): pl.pallas_call(functools.partial(kernel, (ny, nm, coefs, rows, chunks)),...  41.7 us
    pallas_call x1, Pallas kernels, local(): pl.pallas_call(store, out_shape=outs, in_specs=[pl.BlockSpec(memory_space...  1.42 us

profile of v8, /device:TPU:0, one launch (start us, length us, event | category | flops | bytes accessed | tf_op | source)
XLA Modules:
  0.0 44.4 jit_solution(8702742596441251509)
XLA Ops:
  1.3 41.7 %adjoint.1 = (f32[108,4096]{1,0:T(8,128)S(1)}, f32[1024,128]{1,0:T(8,128)S(1)}) custom-call(s32[1]{0:T(128)S(6)} %copy.15.count_smem, s32[128]{0:T(128)} %block_hbm.1, s32[4,512]{1,0:T(4,128)} %neigh_hbm.1, f32[2,108]{1,0:T(2,128)} %tw_hbm.1, f32[4,336,224]{2,1,0:T(8,128)} %constant.2.clone.basis_hbm, f32[54,64,128]{2,1,0:T(8,128)} %bitcast.20, ...), custom_call_target="tpu_custom_call" | custom-call | tf_op jit(solution)/shard_map/adjoint/pallas_call | solution.py:869
  43.0 1.4 %store.1 = (f32[108,4096]{1,0:T(8,128)}, f32[1024,128]{1,0:T(8,128)}) custom-call(f32[108,4096]{1,0:T(8,128)S(1)} %get-tuple-element.6.series, f32[1024,128]{1,0:T(8,128)S(1)} %get-tuple-element.7.state), custom_call_target="tpu_custom_call" | custom-call | tf_op jit(solution)/shard_map/store/pallas_call | solution.py:916

commit v9 on v8

--- a/solution.py
+++ b/solution.py
@@ -216,6 +216,16 @@
                 at_chip(d),
             )
 
+        def send_raw_part(d, r):
+            return remote(
+                spec_hbm.at[:, pl.ds((summed + r) * seg, seg), :],
+                raw.at[d - 1, :, pl.ds(r * seg, seg), :],
+                raw_send.at[d - 1],
+                raw_recv.at[d - 1],
+                "freq",
+                at_chip(d),
+            )
+
         def send_raw_chunk(d, r):
             return remote(
                 own_spec.at[summed + r],
@@ -365,13 +375,16 @@
         @pl.when(other_chip)
         def _():
             pl.semaphore_wait(barrier, jnp.where(first_core, ny, ny - 1))
+
+            @pl.when(other_core)
+            def _():
+                signal(seen.at[chip - 1], "freq", 1)
+
             for d in range(1, ny):
+                send_raw_part(d, 0).start()
                 send_tw(d).start()
-                send_raw(d).start()
-
-        @pl.when(other_core & other_chip)
-        def _():
-            signal(seen.at[chip - 1], "freq", 1)
+                for r in range(1, RAW):
+                    send_raw_part(d, r).start()
 
         load_tw.start()
         for c in (*range(summed, chunks), *range(summed)):

time: 44.5 us -> 44.5 us (level)
  no operation moved by 1% of the time
where the time goes in v9:
time: 44.5 us; the launch traced here: 44.4 us
  Pallas kernels  43.1 us (97%)
  between operations  1.29 us (3%)
    pallas_call x1, Pallas kernels, local(): pl.pallas_call(functools.partial(kernel, (ny, nm, coefs, rows, chunks)),...  41.7 us
    pallas_call x1, Pallas kernels, local(): pl.pallas_call(store, out_shape=outs, in_specs=[pl.BlockSpec(memory_space...  1.42 us

profile of v9, /device:TPU:0, one launch (start us, length us, event | category | flops | bytes accessed | tf_op | source)
XLA Modules:
  0.0 44.4 jit_solution(4943049582295297091)
XLA Ops:
  1.3 41.7 %adjoint.1 = (f32[108,4096]{1,0:T(8,128)S(1)}, f32[1024,128]{1,0:T(8,128)S(1)}) custom-call(s32[1]{0:T(128)S(6)} %copy.15.count_smem, s32[128]{0:T(128)} %block_hbm.1, s32[4,512]{1,0:T(4,128)} %neigh_hbm.1, f32[2,108]{1,0:T(2,128)} %tw_hbm.1, f32[4,336,224]{2,1,0:T(8,128)} %constant.2.clone.basis_hbm, f32[54,64,128]{2,1,0:T(8,128)} %bitcast.20, ...), custom_call_target="tpu_custom_call" | custom-call | tf_op jit(solution)/shard_map/adjoint/pallas_call | solution.py:882
  43.0 1.4 %store.1 = (f32[108,4096]{1,0:T(8,128)}, f32[1024,128]{1,0:T(8,128)}) custom-call(f32[108,4096]{1,0:T(8,128)S(1)} %get-tuple-element.6.series, f32[1024,128]{1,0:T(8,128)S(1)} %get-tuple-element.7.state), custom_call_target="tpu_custom_call" | custom-call | tf_op jit(solution)/shard_map/store/pallas_call | solution.py:929

commit v10 on v9

--- a/solution.py
+++ b/solution.py
@@ -433,8 +433,6 @@
             for o in range(1, nm):
                 signal(barrier, "mesh", peer(o))
 
-        load_coup.start()
-        load_weights.start()
 
         staged[...] = jnp.zeros_like(staged)
         folded[...] = jnp.zeros_like(folded)
@@ -522,6 +520,9 @@
         lax.fori_loop(0, last, send_chunk, 0)
         for d in range(1, ny):
             send_last(d).start()
+
+        load_weights.start()
+        load_coup.start()
 
         def raw_chunk(c, carry):
             @pl.when(c % PAIR == 0)

time: 44.5 us -> 44.5 us (level)
  no operation moved by 1% of the time
where the time goes in v10:
time: 44.5 us; the launch traced here: 44.4 us
  Pallas kernels  43.1 us (97%)
  between operations  1.29 us (3%)
    pallas_call x1, Pallas kernels, local(): pl.pallas_call(functools.partial(kernel, (ny, nm, coefs, rows, chunks)),...  41.7 us
    pallas_call x1, Pallas kernels, local(): pl.pallas_call(store, out_shape=outs, in_specs=[pl.BlockSpec(memory_space...  1.42 us

profile of v10, /device:TPU:0, one launch (start us, length us, event | category | flops | bytes accessed | tf_op | source)
XLA Modules:
  0.0 44.4 jit_solution(1601556699589432521)
XLA Ops:
  1.3 41.7 %adjoint.1 = (f32[108,4096]{1,0:T(8,128)S(1)}, f32[1024,128]{1,0:T(8,128)S(1)}) custom-call(s32[1]{0:T(128)S(6)} %copy.15.count_smem, s32[128]{0:T(128)} %block_hbm.1, s32[4,512]{1,0:T(4,128)} %neigh_hbm.1, f32[2,108]{1,0:T(2,128)} %tw_hbm.1, f32[4,336,224]{2,1,0:T(8,128)} %constant.2.clone.basis_hbm, f32[54,64,128]{2,1,0:T(8,128)} %bitcast.20, ...), custom_call_target="tpu_custom_call" | custom-call | tf_op jit(solution)/shard_map/adjoint/pallas_call | solution.py:883
  43.0 1.4 %store.1 = (f32[108,4096]{1,0:T(8,128)}, f32[1024,128]{1,0:T(8,128)}) custom-call(f32[108,4096]{1,0:T(8,128)S(1)} %get-tuple-element.6.series, f32[1024,128]{1,0:T(8,128)S(1)} %get-tuple-element.7.state), custom_call_target="tpu_custom_call" | custom-call | tf_op jit(solution)/shard_map/store/pallas_call | solution.py:930
